TPU v7x, 512 devices: a 4x2x32 block of a 4x8x32 slice. The times are simulated.
512 devices in a mesh: groups: 2 (over y), rows: 32 (over z), cols: 4 (over x), sub: 2 (over core).
Axes of the slice: x: 4, y: 2, z: 32, core: 2. Of those that a mesh axis runs over, the one named last changes fastest.
The devices are a block of a 4x8x32 slice.
Arguments:
- returns: float32 [8, 512, 8192], P('groups', 'rows', ('cols', 'sub')), parts along dimension 0, may hold values from -6 to 6
- starts: int32 [8, 8192], P('groups', ('cols', 'sub')), parts along dimension 0, may hold values from 0 to 256
- start_block: float32 [8, 32, 8192], P('groups', None, ('cols', 'sub')), parts along dimension 0, may hold values from -6 to 6
Outputs:
- loadings: float32 [8, 32, 8192], P('groups', None, ('cols', 'sub')), parts along dimension 0
There are 2 independent parts, one for each index of `groups`. A program takes and returns all parts, laid end to end along the dimension named above; each array names one. Nothing has to cross between parts.
Inputs may be any that keep to these rules, and one draw needn't show every extreme that they name: `starts`: days before an asset's start day hold returns that do not count.
All inputs are finite; a program needn't handle non-finite values.
Results may differ from a plain program's by a relative error of at most 0.0078.
Values may be sent and summed in bfloat16 or wider, within the bound.
No kernel may reach another device: no remote copies, remote signals or barrier semaphores. Data moves between devices by JAX's collectives and lax.ppermute only.
A program may use at most 64 MiB of HBM per device.

v0:
```python
import jax
import jax.numpy as jnp
from jax import lax
from jax.sharding import PartitionSpec as P

ASSETS = 8192
ITERS = 3


def sent_to_all(array, axis):
    devices = lax.axis_size(axis)
    return lax.all_to_all(
        jnp.broadcast_to(array[None], (devices, *array.shape)), axis, 0, 0, tiled=True
    )


def over_copies(array, axis):
    return sent_to_all(array, axis).sum(axis=0)


def in_one(arrays, axis):
    ends = [0]
    for a in arrays:
        ends.append(ends[-1] + a.size)
    subtotal = over_copies(jnp.concatenate([a.ravel() for a in arrays]), axis)
    return tuple((subtotal[b:e].reshape(a.shape) for a, b, e in zip(arrays, ends, ends[1:])))


def total_of_pieces(array, axis):
    tiles = lax.all_gather(array, axis)
    return tiles.sum(axis=0)


def gram_of(image):
    return jnp.einsum("wkj,wlj->wkl", image, image, precision=lax.Precision.HIGHEST)


def project(factors, scaled):
    rounded = factors.astype(jnp.bfloat16)
    return jnp.einsum("wka,wta->wkt", rounded, scaled, preferred_element_type=jnp.float32)


def expand(proj, widened):
    return jnp.einsum("wkt,wta->wka", proj, widened, precision=lax.Precision.HIGHEST)


def orthonormal(image, gram):
    lower = jnp.linalg.cholesky(gram / ASSETS)
    return jax.scipy.linalg.solve_triangular(lower, image, lower=True)


def on_device(returns, starts, start_block):
    windows, days, width = returns.shape
    rows_count = lax.axis_size("rows")
    row_pos = lax.axis_index("rows")
    total_days = days * rows_count
    day_index = row_pos * days + jnp.arange(days, dtype=jnp.int32)
    live = (day_index[None, :, None] >= starts[:, None, :]).astype(jnp.float32)
    counts = (total_days - starts).astype(jnp.float32)
    masked = live * returns
    sums, powers = in_one((jnp.sum(masked, axis=1), jnp.sum(masked * returns, axis=1)), "rows")
    mean = sums / counts
    centered = live * (returns - mean[:, None, :])
    squares = powers - counts * mean * mean
    scaled = (centered * lax.rsqrt(squares + 1.0)[:, None, :]).astype(jnp.bfloat16)
    widened = scaled.astype(jnp.float32)
    factors = start_block
    for step in range(ITERS):
        proj = over_copies(project(factors, scaled), ("cols", "sub"))
        image = total_of_pieces(expand(proj, widened), "rows")
        gram = over_copies(gram_of(image), ("cols", "sub"))
        factors = orthonormal(image, gram)
    return factors


def solution(mesh):
    placed = (
        P("groups", "rows", ("cols", "sub")),
        P("groups", ("cols", "sub")),
        P("groups", None, ("cols", "sub")),
    )
    return jax.shard_map(
        on_device,
        mesh=mesh,
        in_specs=placed,
        out_specs=P("groups", None, ("cols", "sub")),
        check_vma=False,
    )
```

profile of v0, /device:TPU:40, one launch (start us, length us, event | category | flops | bytes accessed | tf_op | source)
XLA Modules:
  0.0 925.0 jit_solution(15818064703942475469)
XLA Ops:
  6.6 1.1 select_reduce_fusion
  7.7 0.9 broadcast_in_dim.16
  8.7 150.0 %all_to_all.36 = f32[32,1,8192]{2,1,0:T(1,128)S(1)} all-to-all(f32[32,1,8192]{2,1,0:T(1,128)S(1)} %broadcast_in_dim.16), channel_id=1, replica_groups=mesh['groups'=2,'rows'=32,'cols'=4,'sub'=2] {'rows'}, dimensions={0} | all-to-all | bytes 2097152 | tf_op jit(solution)/shard_map/all_to_all | solution.py:12
  158.7 0.7 reduce_sum.110
  159.4 0.7 convert_divide_fusion
  160.2 1.1 fusion.1
  161.3 1.2 convolution_bitcast_fusion
  162.7 10.0 %all_to_all.37 = f32[8,1,2048]{2,1,0:T(1,128)S(1)} all-to-all(f32[8,1,2048]{2,1,0:T(1,128)S(1)} %reshape.57), channel_id=1, replica_groups=mesh['groups'=2,'rows'=32,'cols'=4,'sub'=2] {'cols','sub'}, dimensions={0} | all-to-all | bytes 131072 | tf_op jit(solution)/shard_map/all_to_all | solution.py:12
  172.7 0.5 broadcast.76
  173.2 0.7 reduce.5
  174.1 1.2 fusion.15
  175.3 190.6 %all-gather.7.cloned.1.call-done = f32[128,32,1024]{2,1,0:T(8,128)} async-done(((f32[4,32,1024]{2,1,0:T(8,128)}), f32[128,32,1024]{2,1,0:T(8,128)}) %all-gather.7.cloned.1.call-update) | async-done | bytes 16777232 | tf_op jit(solution)/shard_map/all_gather | solution.py:30
  365.9 7.5 reduce_sum.112
  373.4 0.6 fusion.16
  374.1 0.9 reshape.59
  375.0 4.3 all-to-all-start.2
  379.4 6.0 all-to-all-done.2
  385.4 0.9 reduce.6
  386.7 11.7 %custom-call.10 = f32[4,32,32]{2,1,0:T(8,128)S(1)} custom-call(f32[4,32,32]{2,1,0:T(8,128)S(1)} %fusion.10), custom_call_target="Cholesky" | custom-call | tf_op jit(solution)/shard_map/jit(cholesky)/cholesky | solution.py:48
  398.6 9.8 %custom-call.11 = f32[4,1,32,32]{2,3,1,0:T(8,128)S(1)} custom-call(f32[4,1,32,32]{3,2,1,0:T(8,128)S(1)} %select_bitcast_fusion.2), custom_call_target="InvertDiagBlocksLowerTriangular" | custom-call | tf_op jit(solution)/shard_map/jit(_solve_triangular)/vmap()/triangular_solve | solution.py:49
  408.5 0.7 convolution_convert_fusion.1
  409.1 0.2 fusion.17
  409.5 8.1 all_to_all.38
  417.6 0.7 reduce.7
  418.4 1.2 fusion.18
  419.7 0.2 all-gather.11.cloned.1.call-start
  420.0 201.1 %all-gather.9.cloned.1.call-done = f32[128,32,1024]{2,1,0:T(8,128)} async-done(((f32[4,32,1024]{2,1,0:T(8,128)}), f32[128,32,1024]{2,1,0:T(8,128)}) %all-gather.9.cloned.1.call-update) | async-done | bytes 16777232 | tf_op jit(solution)/shard_map/all_gather | solution.py:30
  621.0 7.5 reduce_sum.115
  628.5 0.6 fusion.19
  629.2 0.3 reshape.63
  629.4 10.2 %all_to_all.39 = f32[8,1,4096]{2,1,0:T(1,128)S(1)} all-to-all(f32[8,1,4096]{2,1,0:T(1,128)S(1)} %reshape.63), channel_id=1, replica_groups=mesh['groups'=2,'rows'=32,'cols'=4,'sub'=2] {'cols','sub'}, dimensions={0} | all-to-all | bytes 262144 | tf_op jit(solution)/shard_map/all_to_all | solution.py:12
  639.6 0.9 reduce.8
  640.9 11.7 %custom-call.12 = f32[4,32,32]{2,1,0:T(8,128)S(1)} custom-call(f32[4,32,32]{2,1,0:T(8,128)S(1)} %fusion.8), custom_call_target="Cholesky" | custom-call | tf_op jit(solution)/shard_map/jit(cholesky)/cholesky | solution.py:48
  652.9 9.8 %custom-call.13 = f32[4,1,32,32]{2,3,1,0:T(8,128)S(1)} custom-call(f32[4,1,32,32]{3,2,1,0:T(8,128)S(1)} %select_bitcast_fusion.1), custom_call_target="InvertDiagBlocksLowerTriangular" | custom-call | tf_op jit(solution)/shard_map/jit(_solve_triangular)/vmap()/triangular_solve | solution.py:49
  662.7 0.7 convolution_convert_fusion
  663.4 0.2 fusion.20
  663.8 8.1 all_to_all.40
  671.8 0.7 reduce.9
  672.7 1.2 fusion.21
  674.0 201.3 %all-gather.11.cloned.1.call-done = f32[128,32,1024]{2,1,0:T(8,128)} async-done(((f32[4,32,1024]{2,1,0:T(8,128)}), f32[128,32,1024]{2,1,0:T(8,128)}) %all-gather.11.cloned.1.call-update) | async-done | bytes 16777232 | tf_op jit(solution)/shard_map/all_gather | solution.py:30
  875.3 7.5 reduce_sum.118
  882.8 0.6 fusion.22
  883.4 0.3 reshape.67
  883.7 10.2 %all_to_all.41 = f32[8,1,4096]{2,1,0:T(1,128)S(1)} all-to-all(f32[8,1,4096]{2,1,0:T(1,128)S(1)} %reshape.67), channel_id=1, replica_groups=mesh['groups'=2,'rows'=32,'cols'=4,'sub'=2] {'cols','sub'}, dimensions={0} | all-to-all | bytes 262144 | tf_op jit(solution)/shard_map/all_to_all | solution.py:12
  893.8 0.9 reduce.10
  895.2 11.7 %custom-call.14 = f32[4,32,32]{2,1,0:T(8,128)S(1)} custom-call(f32[4,32,32]{2,1,0:T(8,128)S(1)} %fusion.6), custom_call_target="Cholesky" | custom-call | tf_op jit(solution)/shard_map/jit(cholesky)/cholesky | solution.py:48
  907.1 9.8 %custom-call.15 = f32[4,1,32,32]{2,3,1,0:T(8,128)S(1)} custom-call(f32[4,1,32,32]{3,2,1,0:T(8,128)S(1)} %select_bitcast_fusion), custom_call_target="InvertDiagBlocksLowerTriangular" | custom-call | tf_op jit(solution)/shard_map/jit(_solve_triangular)/vmap()/triangular_solve | solution.py:49
  917.0 1.4 fusion.4
  (55 shorter events, 3.3 us)
Async XLA Ops:
  6.5 359.4 %all-gather.7.cloned.1.call-start = ((), (), s32[]{:S(2)}) async-start(), calls=%async_computation.7 | async-start | bytes 17301504 | tf_op jit(solution)/shard_map/all_gather | solution.py:30
  375.0 10.4 %all-to-all-start.2 = ((f32[8,1,4096]{2,1,0:T(1,128)}), f32[8,1,4096]{2,1,0:T(1,128)S(1)}, u32[]{:S(2)}, u32[]{:S(2)}) async-start(f32[8,1,4096]{2,1,0:T(1,128)} %reshape.59), calls=%async_computation.2 | async-start | bytes 262144 | tf_op jit(solution)/shard_map/all_to_all | solution.py:12
  379.3 241.8 %all-gather.9.cloned.1.call-start = ((), (), s32[]{:S(2)}) async-start(), calls=%async_computation.8 | async-start | bytes 17301504 | tf_op jit(solution)/shard_map/all_gather | solution.py:30
  419.7 455.6 %all-gather.11.cloned.1.call-start = ((), (), s32[]{:S(2)}) async-start(), calls=%async_computation.9 | async-start | bytes 17301504 | tf_op jit(solution)/shard_map/all_gather | solution.py:30
Sparse Core Ops, SparseCore 0:
  175.4 190.4 all-gather.6
  419.8 201.1 all-gather.8
  674.1 201.1 all-gather.10
where the time goes:
time: 927 us; the launch traced here: 925 us
  waiting for transfers between devices  599 us (65%)
  blocking collectives  197 us (21%)
  other arithmetic  96.5 us (10%)
  between operations  13.5 us (1%)
  matrix products  9.71 us (1%)
    all_gather x3, waiting for transfers between devices, total_of_pieces(): tiles = lax.all_gather(array, axis)  593 us
    all_to_all x6, blocking collectives, sent_to_all(): lax.all_to_all(jnp.broadcast_to(array[None], (devices, *array.shape)), ax...  197 us
    another operation x10, other arithmetic, orthonormal(): lower = jnp.linalg.cholesky(gram / ASSETS)  35.6 us
    another operation x7, other arithmetic, orthonormal(): return jax.scipy.linalg.solve_triangular(lower, image, lower=True)  29.8 us
    reduce_sum x3, other arithmetic, total_of_pieces(): return tiles.sum(axis=0)  22.4 us
  transfers between devices with their start and end apart: 4, of which 4 were waited for; matrix products, arithmetic and copies ran while one was open for 0% of the time, Pallas kernels for 0%

commit v1 on v0

v1 whole, which is shorter than its diff:
```python
import functools

import jax
import jax.numpy as jnp
from jax import lax
from jax.experimental import pallas as pl
from jax.experimental.pallas import tpu as pltpu
from jax.sharding import Mesh
from jax.sharding import PartitionSpec as P

ITERS = 3
LANES = 128
EXTRA = 8
F32 = jnp.float32
BF16 = jnp.bfloat16
HIGHEST = lax.Precision.HIGHEST
VMEM = pl.BlockSpec(memory_space=pltpu.VMEM)
SMEM = pl.BlockSpec(memory_space=pltpu.SMEM)


def dot(a, b, dims, precision=HIGHEST):
    return lax.dot_general(a, b, (dims, ((), ())), precision=precision, preferred_element_type=F32)


def pack_kernel(where_ref, returns_ref, starts_ref, out_ref):
    windows, days, width = returns_ref.shape
    parts = width // LANES
    day = lax.broadcasted_iota(jnp.int32, (days, width), 0) + where_ref[0] * days
    row = lax.broadcasted_iota(jnp.int32, (EXTRA, width), 0)
    for w in range(windows):
        live = day >= starts_ref[w : w + 1, :]
        kept = jnp.where(live, returns_ref[w], 0.0)
        number = jnp.sum(live.astype(F32), axis=0, keepdims=True)
        shift = jnp.sum(kept, axis=0, keepdims=True) / jnp.maximum(number, 1.0)
        high = shift.astype(BF16).astype(F32)
        middle = (shift - high).astype(BF16).astype(F32)
        low = (shift - high - middle).astype(BF16).astype(F32)
        shift = high + middle + low
        rest = jnp.where(live, kept - shift, 0.0).astype(BF16)
        carried = jnp.where(row == 0, high, jnp.where(row == 1, middle, jnp.where(row == 2, low, 0.0))).astype(BF16)
        for j in range(parts):
            at = slice(j * LANES, (j + 1) * LANES)
            out_ref[w * parts + j, 0:days, :] = rest[:, at]
            out_ref[w * parts + j, days : days + EXTRA, :] = carried[:, at]


def tiles_of(days):
    blocks = days // LANES
    return [(a, b) for a in range(blocks) for b in range(a, blocks)]


def gram_kernel(where_ref, got_ref, starts_ref, block_ref, scaled_ref, out_ref):
    sources, rows, _ = got_ref.shape
    days = rows - EXTRA
    total = sources * days
    w = where_ref[0]
    starts = starts_ref[pl.ds(w, 1), :]
    got = got_ref[...].astype(F32)
    shift = jnp.sum(got[:, days:, :], axis=1, keepdims=True)
    values = (got[:, :days, :] + shift).reshape(total, LANES)
    live = lax.broadcasted_iota(jnp.int32, (total, LANES), 0) >= starts
    counts = (total - starts).astype(F32)
    mean = jnp.sum(jnp.where(live, values, 0.0), axis=0, keepdims=True) / counts
    centered = jnp.where(live, values - mean, 0.0)
    squares = jnp.sum(centered * centered, axis=0, keepdims=True)
    scaled = centered * lax.rsqrt(squares + 1.0)
    scaled_ref[...] = scaled
    blocks = total // LANES
    at = 0
    for a in range(blocks):
        strip = dot(scaled[a * LANES : (a + 1) * LANES], scaled[a * LANES :], ((1,), (1,)))
        for b in range(a, blocks):
            out_ref[at : at + LANES, :] = strip[:, (b - a) * LANES : (b - a + 1) * LANES]
            at += LANES
    rounded = block_ref[0].astype(BF16).astype(F32)
    proj = dot(rounded, scaled, ((1,), (1,)))
    factors = proj.shape[0]
    for b in range(blocks):
        out_ref[at : at + factors, :] = proj[:, b * LANES : (b + 1) * LANES]
        at += factors
    if at < out_ref.shape[0]:
        out_ref[at:, :] = jnp.zeros((out_ref.shape[0] - at, LANES), F32)


def inverse_lower(gram):
    k = gram.shape[0]
    row = lax.broadcasted_iota(jnp.int32, (k, LANES), 0)
    lane = lax.broadcasted_iota(jnp.int32, (k, LANES), 1)
    both = jnp.concatenate([gram, jnp.zeros((k, LANES - k), F32)], axis=1)
    both = jnp.where(lane == row + k, 1.0, both)
    for i in range(k - 1):
        column = jnp.where(row > i, both[:, i : i + 1], 0.0)
        line = both[i : i + 1, :]
        both = both - column * (line / both[i : i + 1, i : i + 1])
    pivots = jnp.sum(jnp.where(lane == row, both, 0.0), axis=1, keepdims=True)
    return (both * lax.rsqrt(pivots))[:, k : 2 * k]


def iterate_kernel(assets, got_ref, scaled_ref, out_ref, gram_ref):
    total = scaled_ref.shape[0]
    factors = out_ref.shape[1]
    blocks = total // LANES
    at = 0
    for a, b in tiles_of(total):
        tile = got_ref[at : at + LANES, :]
        gram_ref[a * LANES : (a + 1) * LANES, b * LANES : (b + 1) * LANES] = tile
        if a != b:
            gram_ref[b * LANES : (b + 1) * LANES, a * LANES : (a + 1) * LANES] = tile.T
        at += LANES
    proj = jnp.concatenate([got_ref[at + b * factors : at + (b + 1) * factors, :] for b in range(blocks)], axis=1)
    for step in range(ITERS):
        moved = dot(proj, gram_ref[...], ((1,), (0,)))
        gram = dot(moved, proj, ((1,), (1,))) * (1.0 / assets)
        inverse = inverse_lower(gram)
        proj = dot(inverse, moved if step < ITERS - 1 else proj, ((1,), (0,)))
    loadings = dot(proj, scaled_ref[...], ((1,), (0,))).astype(BF16)
    out_ref[...] = jnp.broadcast_to(loadings[None], out_ref.shape)


def unpack_kernel(got_ref, out_ref):
    windows, _, width = out_ref.shape
    parts = width // LANES
    for w in range(windows):
        for j in range(parts):
            out_ref[w, :, j * LANES : (j + 1) * LANES] = got_ref[w * parts + j].astype(F32)


def on_device(returns, starts, start_block):
    windows, days, width = returns.shape
    factors = start_block.shape[1]
    parts = width // LANES
    rows = windows * parts
    sides = lax.axis_size(("cols", "sub"))
    total = days * rows
    assets = width * sides
    w, j = lax.axis_index("window"), lax.axis_index("part")
    row = w * parts + j

    packed = pl.pallas_call(
        pack_kernel,
        out_shape=jax.ShapeDtypeStruct((rows, days + EXTRA, LANES), BF16),
        in_specs=[SMEM, VMEM, VMEM],
        out_specs=VMEM,
        name="pack",
    )(row[None], returns, starts)
    got = lax.all_to_all(packed, ("window", "part"), 0, 0, tiled=True)

    filled = len(tiles_of(total)) * LANES + factors * total // LANES
    unit = 8 * sides * parts
    height = (filled + unit - 1) // unit * unit
    scaled, partial = pl.pallas_call(
        gram_kernel,
        out_shape=(
            jax.ShapeDtypeStruct((total, LANES), F32),
            jax.ShapeDtypeStruct((height, LANES), F32),
        ),
        grid_spec=pltpu.PrefetchScalarGridSpec(
            num_scalar_prefetch=1,
            grid=(1,),
            in_specs=[
                pl.BlockSpec((rows, days + EXTRA, LANES), lambda g, s: (0, 0, 0)),
                pl.BlockSpec((windows, LANES), lambda g, s: (0, s[1])),
                pl.BlockSpec((1, factors, LANES), lambda g, s: (s[0], 0, s[1])),
            ],
            out_specs=(
                pl.BlockSpec((total, LANES), lambda g, s: (0, 0)),
                pl.BlockSpec((height, LANES), lambda g, s: (0, 0)),
            ),
        ),
        name="gram",
    )(jnp.stack([w, j]), got, starts, start_block)

    own = lax.all_to_all(partial.reshape(sides, height // sides, LANES), ("cols", "sub"), 0, 0, tiled=True)
    own = own.sum(axis=0).reshape(parts, height // sides // parts, LANES)
    own = lax.all_to_all(own, "part", 0, 0, tiled=True).sum(axis=0)
    own = lax.all_to_all(jnp.broadcast_to(own[None], (parts, *own.shape)), "part", 0, 0, tiled=True)
    whole = lax.all_gather(own.reshape(height // sides, LANES), ("cols", "sub"), tiled=True)

    sent = pl.pallas_call(
        functools.partial(iterate_kernel, assets),
        out_shape=jax.ShapeDtypeStruct((rows, factors, LANES), BF16),
        in_specs=[VMEM, VMEM],
        out_specs=VMEM,
        scratch_shapes=[pltpu.VMEM((total, total), F32)],
        name="iterate",
    )(whole, scaled)
    got = lax.all_to_all(sent, ("window", "part"), 0, 0, tiled=True)
    return pl.pallas_call(
        unpack_kernel,
        out_shape=jax.ShapeDtypeStruct((windows, factors, width), F32),
        in_specs=[VMEM],
        out_specs=VMEM,
        name="unpack",
    )(got)


def solution(mesh):
    groups, rows, cols, sub = (mesh.shape[name] for name in ("groups", "rows", "cols", "sub"))

    def whole(returns, starts, start_block):
        windows = returns.shape[0] // groups
        split = Mesh(
            mesh.devices.reshape(groups, windows, rows // windows, cols, sub),
            ("groups", "window", "part", "cols", "sub"),
        )
        placed = (
            P("groups", ("window", "part"), ("cols", "sub")),
            P("groups", ("cols", "sub")),
            P("groups", None, ("cols", "sub")),
        )
        return jax.shard_map(
            on_device,
            mesh=split,
            in_specs=placed,
            out_specs=P("groups", None, ("cols", "sub")),
            check_vma=False,
        )(returns, starts, start_block)

    return whole
```

time: 927 us -> 215 us (0.23)
  waiting for transfers between devices: 599 us -> 35.7 us
  other arithmetic: 96.5 us -> 0.71 us
  blocking collectives: 197 us -> 111 us
  starting transfers between devices: 4.59 us -> 45.8 us
  Pallas kernels: 0 us -> 20.4 us
  between operations: 13.5 us -> 0.03 us
  matrix products: 9.71 us -> 0 us
    all_gather x3 -> x0, waiting for transfers between devices: 593 us -> none  [total_of_pieces(): tiles = lax.all_gather(array, axis)]
    all_to_all x6 -> x4, blocking collectives: 197 us -> 97 us  [the longest x1 51 us: on_device(): got = lax.all_to_all(sent, ('window', 'part'), 0, 0, tiled=True)]
    another operation x17 -> x1, other arithmetic: 65.4 us -> 0.65 us  [on_device(): jnp.stack([w, j])]
    all_to_all x1, starting transfers between devices: 4.28 us -> 45.8 us  [on_device(): got = lax.all_to_all(packed, ('window', 'part'), 0, 0, tiled=True)]
    all_to_all x1, waiting for transfers between devices: 6.01 us -> 35.7 us  [on_device(): got = lax.all_to_all(packed, ('window', 'part'), 0, 0, tiled=True)]
    reduce_sum x11 -> x2, other arithmetic: 24.4 us -> 0.05 us  [the longest x1 0.04 us: on_device(): own = own.sum(axis=0).reshape(parts, height // sides // parts, LANES)]
    pallas_call x0 -> x4, Pallas kernels: none -> 20.4 us  [the longest x1 13.1 us: on_device(): pl.pallas_call(functools.partial(iterate_kernel, assets), out_shape=jax.S...]
    all_gather x0 -> x1, blocking collectives: none -> 14.5 us  [on_device(): lax.all_gather(own.reshape(height // sides, LANES), ('cols', 'sub'), tile...]
  transfers between devices with their start and end apart: 4 -> 1, of which waited for: 4 -> 1; matrix products, arithmetic and copies ran while one was open for 0% -> 0% of each run, Pallas kernels for 0% -> 0%
where the time goes in v1:
time: 215 us
  blocking collectives  111 us (52%)
  starting transfers between devices  45.8 us (21%)
  waiting for transfers between devices  35.7 us (17%)
  Pallas kernels  20.4 us (9%)
    all_to_all x1, blocking collectives, on_device(): got = lax.all_to_all(sent, ('window', 'part'), 0, 0, tiled=True)  51 us
    all_to_all x1, starting transfers between devices, on_device(): got = lax.all_to_all(packed, ('window', 'part'), 0, 0, tiled=True)  45.8 us
    all_to_all x1, waiting for transfers between devices, on_device(): got = lax.all_to_all(packed, ('window', 'part'), 0, 0, tiled=True)  35.7 us
    all_to_all x1, blocking collectives, on_device(): lax.all_to_all(partial.reshape(sides, height // sides, LANES), ('cols', '...  17.7 us
    all_gather x1, blocking collectives, on_device(): lax.all_gather(own.reshape(height // sides, LANES), ('cols', 'sub'), tile...  14.5 us
    all_to_all x1, blocking collectives, on_device(): lax.all_to_all(jnp.broadcast_to(own[None], (parts, *own.shape)), 'part',...  14.5 us
    all_to_all x1, blocking collectives, on_device(): own = lax.all_to_all(own, 'part', 0, 0, tiled=True).sum(axis=0)  13.7 us
    pallas_call x1, Pallas kernels, on_device(): pl.pallas_call(functools.partial(iterate_kernel, assets), out_shape=jax.S...  13.1 us
  transfers between devices with their start and end apart: 1, of which 1 were waited for; matrix products, arithmetic and copies ran while one was open for 0% of the time, Pallas kernels for 0%

profile of v1, /device:TPU:40, one launch (start us, length us, event | category | flops | bytes accessed | tf_op | source)
XLA Modules:
  0.0 214.8 jit_solution(8165074577011671459)
XLA Ops:
  0.0 1.8 pack.1
  1.8 45.8 %all-to-all-start = ((bf16[32,24,128]{2,1,0:T(8,128)(2,1)}), bf16[32,24,128]{2,1,0:T(8,128)(2,1)S(1)}, u32[]{:S(2)}, u32[]{:S(2)}) async-start(bf16[32,24,128]{2,1,0:T(8,128)(2,1)} %pack.1), calls=%async_computation | async-start | bytes 393216 | tf_op jit(solution)/shard_map/all_to_all | solution.py:146
  47.6 0.7 pad_add_fusion.where_ref
  48.2 35.7 %all-to-all-done.got_ref = bf16[32,24,128]{2,1,0:T(8,128)(2,1)S(1)} async-done(((bf16[32,24,128]{2,1,0:T(8,128)(2,1)}), bf16[32,24,128]{2,1,0:T(8,128)(2,1)S(1)}, u32[]{:S(2)}, u32[]{:S(2)}) %all-to-all-start) | async-done | bytes 196640 | tf_op jit(solution)/shard_map/all_to_all | solution.py:146
  84.0 0.0 copy-start
  84.0 0.7 copy-done
  84.6 3.7 %gram.1 = (f32[512,128]{1,0:T(8,128)}, f32[1536,128]{1,0:T(8,128)}) custom-call(s32[2]{0:T(128)} %pad_add_fusion.where_ref, bf16[32,24,128]{2,1,0:T(8,128)(2,1)} %copy-done, s32[4,1024]{1,0:T(4,128)} %starts_ref.3, f32[4,32,1024]{2,1,0:T(8,128)} %block_ref.1), custom_call_target="tpu_custom_call" | custom-call | tf_op jit(solution)/shard_map/gram/pallas_call | solution.py:151
  88.4 17.7 %all_to_all.25 = f32[8,192,128]{2,1,0:T(8,128)S(1)} all-to-all(f32[8,192,128]{2,1,0:T(8,128)} %bitcast.6), channel_id=1, replica_groups=mesh['groups'=2,'window'=4,'part'=8,'cols'=4,'sub'=2] {'cols','sub'}, dimensions={0} | all-to-all | bytes 1572864 | tf_op jit(solution)/shard_map/all_to_all | solution.py:173
  106.2 13.7 %all_to_all.26 = f32[8,24,128]{2,1,0:T(8,128)S(1)} all-to-all(f32[8,24,128]{2,1,0:T(8,128)S(1)} %bitcast.7), channel_id=1, replica_groups=mesh['groups'=2,'window'=4,'part'=8,'cols'=4,'sub'=2] {'part'}, dimensions={0} | all-to-all | bytes 196608 | tf_op jit(solution)/shard_map/all_to_all | solution.py:175
  119.9 14.5 %all_to_all.27 = f32[8,24,128]{2,1,0:T(8,128)S(1)} all-to-all(f32[8,24,128]{2,1,0:T(8,128)S(1)} %broadcast_in_dim.10), channel_id=1, replica_groups=mesh['groups'=2,'window'=4,'part'=8,'cols'=4,'sub'=2] {'part'}, dimensions={0} | all-to-all | bytes 196608 | tf_op jit(solution)/shard_map/all_to_all | solution.py:176
  134.4 14.5 %all_gather.3.got_ref = f32[1536,128]{1,0:T(8,128)} all-gather(f32[192,128]{1,0:T(8,128)S(1)} %bitcast.8), channel_id=1, replica_groups=mesh['groups'=2,'window'=4,'part'=8,'cols'=4,'sub'=2] {'cols','sub'}, dimensions={0}, use_global_device_ids=true | all-gather | bytes 884736 | tf_op jit(solution)/shard_map/all_gather | solution.py:177
  148.9 13.1 %iterate.1 = bf16[32,32,128]{2,1,0:T(8,128)(2,1)} custom-call(f32[1536,128]{1,0:T(8,128)} %all_gather.3.got_ref, f32[512,128]{1,0:T(8,128)} %get-tuple-element.8.scaled_ref), custom_call_target="tpu_custom_call" | custom-call | tf_op jit(solution)/shard_map/iterate/pallas_call | solution.py:179
  162.0 51.0 %all_to_all.28.got_ref = bf16[32,32,128]{2,1,0:T(8,128)(2,1)} all-to-all(bf16[32,32,128]{2,1,0:T(8,128)(2,1)} %iterate.1), channel_id=1, replica_groups=mesh['groups'=2,'window'=4,'part'=8,'cols'=4,'sub'=2] {'window','part'}, dimensions={0} | all-to-all | bytes 524288 | tf_op jit(solution)/shard_map/all_to_all | solution.py:187
  213.0 1.8 unpack.1
  (3 shorter events, 0.1 us)
Async XLA Ops:
  1.8 82.1 %all-to-all-start = ((bf16[32,24,128]{2,1,0:T(8,128)(2,1)}), bf16[32,24,128]{2,1,0:T(8,128)(2,1)S(1)}, u32[]{:S(2)}, u32[]{:S(2)}) async-start(bf16[32,24,128]{2,1,0:T(8,128)(2,1)} %pack.1), calls=%async_computation | async-start | bytes 393216 | tf_op jit(solution)/shard_map/all_to_all | solution.py:146
  84.0 0.7 copy-start

commit v2 on v1

--- a/solution.py
+++ b/solution.py
@@ -16,10 +16,21 @@
 HIGHEST = lax.Precision.HIGHEST
 VMEM = pl.BlockSpec(memory_space=pltpu.VMEM)
 SMEM = pl.BlockSpec(memory_space=pltpu.SMEM)
+PARAMS = pltpu.CompilerParams(vmem_limit_bytes=16 << 20)
 
 
 def dot(a, b, dims, precision=HIGHEST):
     return lax.dot_general(a, b, (dims, ((), ())), precision=precision, preferred_element_type=F32)
+
+
+def split(a):
+    high = a.astype(BF16)
+    return high, (a - high.astype(F32)).astype(BF16)
+
+
+def dot3(a, b, dims):
+    (ah, al), (bh, bl) = split(a), split(b)
+    return dot(ah, bh, dims, None) + (dot(al, bh, dims, None) + dot(ah, bl, dims, None))
 
 
 def pack_kernel(where_ref, returns_ref, starts_ref, out_ref):
@@ -49,12 +60,11 @@
     return [(a, b) for a in range(blocks) for b in range(a, blocks)]
 
 
-def gram_kernel(where_ref, got_ref, starts_ref, block_ref, scaled_ref, out_ref):
+def gram_kernel(got_ref, starts_ref, block_ref, scaled_ref, out_ref):
     sources, rows, _ = got_ref.shape
     days = rows - EXTRA
     total = sources * days
-    w = where_ref[0]
-    starts = starts_ref[pl.ds(w, 1), :]
+    starts = starts_ref[...]
     got = got_ref[...].astype(F32)
     shift = jnp.sum(got[:, days:, :], axis=1, keepdims=True)
     values = (got[:, :days, :] + shift).reshape(total, LANES)
@@ -65,15 +75,19 @@
     squares = jnp.sum(centered * centered, axis=0, keepdims=True)
     scaled = centered * lax.rsqrt(squares + 1.0)
     scaled_ref[...] = scaled
+    high, low = split(scaled)
     blocks = total // LANES
+    across = ((1,), (1,))
     at = 0
     for a in range(blocks):
-        strip = dot(scaled[a * LANES : (a + 1) * LANES], scaled[a * LANES :], ((1,), (1,)))
+        here, on = slice(a * LANES, (a + 1) * LANES), slice(a * LANES, total)
+        strip = dot(high[here], high[on], across, None)
+        strip += dot(low[here], high[on], across, None) + dot(high[here], low[on], across, None)
         for b in range(a, blocks):
             out_ref[at : at + LANES, :] = strip[:, (b - a) * LANES : (b - a + 1) * LANES]
             at += LANES
-    rounded = block_ref[0].astype(BF16).astype(F32)
-    proj = dot(rounded, scaled, ((1,), (1,)))
+    rounded = block_ref[...].astype(BF16)
+    proj = dot(rounded, high, across, None) + dot(rounded, low, across, None)
     factors = proj.shape[0]
     for b in range(blocks):
         out_ref[at : at + factors, :] = proj[:, b * LANES : (b + 1) * LANES]
@@ -84,36 +98,53 @@
 
 def inverse_lower(gram):
     k = gram.shape[0]
+    size = 8
     row = lax.broadcasted_iota(jnp.int32, (k, LANES), 0)
     lane = lax.broadcasted_iota(jnp.int32, (k, LANES), 1)
     both = jnp.concatenate([gram, jnp.zeros((k, LANES - k), F32)], axis=1)
     both = jnp.where(lane == row + k, 1.0, both)
-    for i in range(k - 1):
-        column = jnp.where(row > i, both[:, i : i + 1], 0.0)
-        line = both[i : i + 1, :]
-        both = both - column * (line / both[i : i + 1, i : i + 1])
+    for i in range(0, k, size):
+        columns = [jnp.broadcast_to(both[:, i + q : i + q + 1], (k, LANES)) for q in range(size)]
+        lines = [both[i + q : i + q + 1, :] for q in range(size)]
+        inner = {(q, p): columns[q][i + p : i + p + 1, :] for q in range(size) for p in range(q, size)}
+        update = jnp.zeros((k, LANES), F32)
+        for q in range(size):
+            inverse = 1.0 / inner[q, q]
+            later = range(q + 1, size)
+            ratio = {p: inner[q, p] * inverse for p in later}
+            for p in later:
+                for r in range(p, size):
+                    inner[p, r] -= ratio[p] * inner[q, r]
+            for p in later:
+                lines[p] -= ratio[p] * lines[q]
+                columns[p] -= columns[q] * ratio[p]
+            update += jnp.where(row > i + q, columns[q] * inverse, 0.0) * lines[q]
+        both -= update
     pivots = jnp.sum(jnp.where(lane == row, both, 0.0), axis=1, keepdims=True)
     return (both * lax.rsqrt(pivots))[:, k : 2 * k]
 
 
-def iterate_kernel(assets, got_ref, scaled_ref, out_ref, gram_ref):
+def iterate_kernel(assets, got_ref, scaled_ref, out_ref, high_ref, low_ref):
     total = scaled_ref.shape[0]
     factors = out_ref.shape[1]
     blocks = total // LANES
     at = 0
     for a, b in tiles_of(total):
+        rows, columns = slice(a * LANES, (a + 1) * LANES), slice(b * LANES, (b + 1) * LANES)
         tile = got_ref[at : at + LANES, :]
-        gram_ref[a * LANES : (a + 1) * LANES, b * LANES : (b + 1) * LANES] = tile
+        high_ref[rows, columns], low_ref[rows, columns] = split(tile)
         if a != b:
-            gram_ref[b * LANES : (b + 1) * LANES, a * LANES : (a + 1) * LANES] = tile.T
+            high_ref[columns, rows], low_ref[columns, rows] = split(tile.T)
         at += LANES
     proj = jnp.concatenate([got_ref[at + b * factors : at + (b + 1) * factors, :] for b in range(blocks)], axis=1)
+    inward = ((1,), (0,))
     for step in range(ITERS):
-        moved = dot(proj, gram_ref[...], ((1,), (0,)))
+        high, low = split(proj)
+        stacked = dot(jnp.concatenate([high, low], axis=0), high_ref[...], inward, None)
+        moved = stacked[:factors] + (stacked[factors:] + dot(high, low_ref[...], inward, None))
         gram = dot(moved, proj, ((1,), (1,))) * (1.0 / assets)
-        inverse = inverse_lower(gram)
-        proj = dot(inverse, moved if step < ITERS - 1 else proj, ((1,), (0,)))
-    loadings = dot(proj, scaled_ref[...], ((1,), (0,))).astype(BF16)
+        proj = dot(inverse_lower(gram), moved if step < ITERS - 1 else proj, inward)
+    loadings = dot3(proj, scaled_ref[...], inward).astype(BF16)
     out_ref[...] = jnp.broadcast_to(loadings[None], out_ref.shape)
 
 
@@ -141,6 +172,7 @@
         out_shape=jax.ShapeDtypeStruct((rows, days + EXTRA, LANES), BF16),
         in_specs=[SMEM, VMEM, VMEM],
         out_specs=VMEM,
+        compiler_params=PARAMS,
         name="pack",
     )(row[None], returns, starts)
     got = lax.all_to_all(packed, ("window", "part"), 0, 0, tiled=True)
@@ -154,21 +186,15 @@
             jax.ShapeDtypeStruct((total, LANES), F32),
             jax.ShapeDtypeStruct((height, LANES), F32),
         ),
-        grid_spec=pltpu.PrefetchScalarGridSpec(
-            num_scalar_prefetch=1,
-            grid=(1,),
-            in_specs=[
-                pl.BlockSpec((rows, days + EXTRA, LANES), lambda g, s: (0, 0, 0)),
-                pl.BlockSpec((windows, LANES), lambda g, s: (0, s[1])),
-                pl.BlockSpec((1, factors, LANES), lambda g, s: (s[0], 0, s[1])),
-            ],
-            out_specs=(
-                pl.BlockSpec((total, LANES), lambda g, s: (0, 0)),
-                pl.BlockSpec((height, LANES), lambda g, s: (0, 0)),
-            ),
-        ),
+        in_specs=[VMEM] * 3,
+        out_specs=(VMEM, VMEM),
+        compiler_params=PARAMS,
         name="gram",
-    )(jnp.stack([w, j]), got, starts, start_block)
+    )(
+        got,
+        lax.dynamic_slice(starts, (w, j * LANES), (1, LANES)),
+        lax.dynamic_slice(start_block, (w, 0, j * LANES), (1, factors, LANES))[0],
+    )
 
     own = lax.all_to_all(partial.reshape(sides, height // sides, LANES), ("cols", "sub"), 0, 0, tiled=True)
     own = own.sum(axis=0).reshape(parts, height // sides // parts, LANES)
@@ -181,7 +207,8 @@
         out_shape=jax.ShapeDtypeStruct((rows, factors, LANES), BF16),
         in_specs=[VMEM, VMEM],
         out_specs=VMEM,
-        scratch_shapes=[pltpu.VMEM((total, total), F32)],
+        scratch_shapes=[pltpu.VMEM((total, total), BF16)] * 2,
+        compiler_params=PARAMS,
         name="iterate",
     )(whole, scaled)
     got = lax.all_to_all(sent, ("window", "part"), 0, 0, tiled=True)
@@ -190,6 +217,7 @@
         out_shape=jax.ShapeDtypeStruct((windows, factors, width), F32),
         in_specs=[VMEM],
         out_specs=VMEM,
+        compiler_params=PARAMS,
         name="unpack",
     )(got)
 

time: 215 us -> 202 us (0.940)
  Pallas kernels: 20.4 us -> 7.25 us
    pallas_call x1, Pallas kernels: 13.1 us -> 4.82 us  [on_device(): pl.pallas_call(functools.partial(iterate_kernel, assets), out_shape=jax.S...]
    pallas_call x1, Pallas kernels: 3.72 us -> 0.73 us  [on_device(): pl.pallas_call(gram_kernel, out_shape=(jax.ShapeDtypeStruct((total, LANES...]
where the time goes in v2:
time: 202 us; the launch traced here: 201 us
  blocking collectives  110 us (54%)
  starting transfers between devices  45.8 us (23%)
  waiting for transfers between devices  36.3 us (18%)
  Pallas kernels  7.25 us (4%)
    all_to_all x1, blocking collectives, on_device(): got = lax.all_to_all(sent, ('window', 'part'), 0, 0, tiled=True)  50.7 us
    all_to_all x1, starting transfers between devices, on_device(): got = lax.all_to_all(packed, ('window', 'part'), 0, 0, tiled=True)  45.8 us
    all_to_all x1, waiting for transfers between devices, on_device(): got = lax.all_to_all(packed, ('window', 'part'), 0, 0, tiled=True)  36.3 us
    all_to_all x1, blocking collectives, on_device(): lax.all_to_all(partial.reshape(sides, height // sides, LANES), ('cols', '...  17.5 us
    all_to_all x1, blocking collectives, on_device(): lax.all_to_all(jnp.broadcast_to(own[None], (parts, *own.shape)), 'part',...  14.5 us
    all_to_all x1, blocking collectives, on_device(): own = lax.all_to_all(own, 'part', 0, 0, tiled=True).sum(axis=0)  13.7 us
    all_gather x1, blocking collectives, on_device(): lax.all_gather(own.reshape(height // sides, LANES), ('cols', 'sub'), tile...  13.4 us
    pallas_call x1, Pallas kernels, on_device(): pl.pallas_call(functools.partial(iterate_kernel, assets), out_shape=jax.S...  4.82 us
  transfers between devices with their start and end apart: 1, of which 1 were waited for; matrix products, arithmetic and copies ran while one was open for 0% of the time, Pallas kernels for 0%

profile of v2, /device:TPU:40, one launch (start us, length us, event | category | flops | bytes accessed | tf_op | source)
XLA Modules:
  0.0 201.1 jit_solution(3562434094027515614)
XLA Ops:
  0.0 0.0 copy-start
  0.0 0.0 copy-start.2
  0.0 0.8 copy-done.2
  0.8 0.0 copy-start.1
  0.8 0.9 copy-done.1
  1.7 0.9 pack.1
  2.6 45.8 %all-to-all-start = ((bf16[32,24,128]{2,1,0:T(8,128)(2,1)}), bf16[32,24,128]{2,1,0:T(8,128)(2,1)S(1)}, u32[]{:S(2)}, u32[]{:S(2)}) async-start(bf16[32,24,128]{2,1,0:T(8,128)(2,1)} %pack.1), calls=%async_computation | async-start | bytes 393216 | tf_op jit(solution)/shard_map/all_to_all | solution.py:178
  48.4 0.1 dynamic_slice.6.starts_ref
  48.5 0.0 copy-done
  48.5 36.3 %all-to-all-done.got_ref = bf16[32,24,128]{2,1,0:T(8,128)(2,1)S(1)} async-done(((bf16[32,24,128]{2,1,0:T(8,128)(2,1)}), bf16[32,24,128]{2,1,0:T(8,128)(2,1)S(1)}, u32[]{:S(2)}, u32[]{:S(2)}) %all-to-all-start) | async-done | bytes 196640 | tf_op jit(solution)/shard_map/all_to_all | solution.py:178
  84.7 0.7 gram.1
  85.5 17.5 %all_to_all.25 = f32[8,192,128]{2,1,0:T(8,128)S(1)} all-to-all(f32[8,192,128]{2,1,0:T(8,128)S(1)} %bitcast.6), channel_id=1, replica_groups=mesh['groups'=2,'window'=4,'part'=8,'cols'=4,'sub'=2] {'cols','sub'}, dimensions={0} | all-to-all | bytes 1572864 | tf_op jit(solution)/shard_map/all_to_all | solution.py:199
  103.1 13.7 %all_to_all.26 = f32[8,24,128]{2,1,0:T(8,128)S(1)} all-to-all(f32[8,24,128]{2,1,0:T(8,128)S(1)} %bitcast.7), channel_id=1, replica_groups=mesh['groups'=2,'window'=4,'part'=8,'cols'=4,'sub'=2] {'part'}, dimensions={0} | all-to-all | bytes 196608 | tf_op jit(solution)/shard_map/all_to_all | solution.py:201
  116.8 14.5 %all_to_all.27 = f32[8,24,128]{2,1,0:T(8,128)S(1)} all-to-all(f32[8,24,128]{2,1,0:T(8,128)S(1)} %broadcast_in_dim.10), channel_id=1, replica_groups=mesh['groups'=2,'window'=4,'part'=8,'cols'=4,'sub'=2] {'part'}, dimensions={0} | all-to-all | bytes 196608 | tf_op jit(solution)/shard_map/all_to_all | solution.py:202
  131.3 13.4 %all_gather.3.got_ref = f32[1536,128]{1,0:T(8,128)S(1)} all-gather(f32[192,128]{1,0:T(8,128)S(1)} %bitcast.8), channel_id=1, replica_groups=mesh['groups'=2,'window'=4,'part'=8,'cols'=4,'sub'=2] {'cols','sub'}, dimensions={0}, use_global_device_ids=true | all-gather | bytes 884736 | tf_op jit(solution)/shard_map/all_gather | solution.py:203
  144.7 4.8 %iterate.1 = bf16[32,32,128]{2,1,0:T(8,128)(2,1)S(1)} custom-call(f32[1536,128]{1,0:T(8,128)S(1)} %all_gather.3.got_ref, f32[512,128]{1,0:T(8,128)S(1)} %get-tuple-element.8.scaled_ref), custom_call_target="tpu_custom_call" | custom-call | tf_op jit(solution)/shard_map/iterate/pallas_call | solution.py:205
  149.6 50.7 %all_to_all.28.got_ref = bf16[32,32,128]{2,1,0:T(8,128)(2,1)S(1)} all-to-all(bf16[32,32,128]{2,1,0:T(8,128)(2,1)S(1)} %iterate.1), channel_id=1, replica_groups=mesh['groups'=2,'window'=4,'part'=8,'cols'=4,'sub'=2] {'window','part'}, dimensions={0} | all-to-all | bytes 524288 | tf_op jit(solution)/shard_map/all_to_all | solution.py:214
  200.3 0.8 unpack.1
  (4 shorter events, 0.1 us)
Async XLA Ops:
  0.0 48.5 %copy-start = (f32[4,32,1024]{2,1,0:T(8,128)S(1)}, f32[4,32,1024]{2,1,0:T(8,128)}, u32[]{:S(2)}) copy-start(f32[4,32,1024]{2,1,0:T(8,128)} %param.5) | copy-start | bytes 1572868
  0.0 0.8 copy-start.2
  0.8 0.9 copy-start.1
  2.6 82.1 %all-to-all-start = ((bf16[32,24,128]{2,1,0:T(8,128)(2,1)}), bf16[32,24,128]{2,1,0:T(8,128)(2,1)S(1)}, u32[]{:S(2)}, u32[]{:S(2)}) async-start(bf16[32,24,128]{2,1,0:T(8,128)(2,1)} %pack.1), calls=%async_computation | async-start | bytes 393216 | tf_op jit(solution)/shard_map/all_to_all | solution.py:178

commit v3 on v2

--- a/solution.py
+++ b/solution.py
@@ -10,6 +10,8 @@
 
 ITERS = 3
 LANES = 128
+HALF = LANES // 2
+NEAR = 4
 EXTRA = 8
 F32 = jnp.float32
 BF16 = jnp.bfloat16
@@ -55,11 +57,6 @@
             out_ref[w * parts + j, days : days + EXTRA, :] = carried[:, at]
 
 
-def tiles_of(days):
-    blocks = days // LANES
-    return [(a, b) for a in range(blocks) for b in range(a, blocks)]
-
-
 def gram_kernel(got_ref, starts_ref, block_ref, scaled_ref, out_ref):
     sources, rows, _ = got_ref.shape
     days = rows - EXTRA
@@ -78,20 +75,29 @@
     high, low = split(scaled)
     blocks = total // LANES
     across = ((1,), (1,))
+    rounded = block_ref[...].astype(BF16)
+    proj = dot(rounded, high, across, None) + dot(rounded, low, across, None)
+    rest = []
     at = 0
+
+    def put(tile):
+        nonlocal at
+        out_ref[at : at + tile.shape[0], :] = tile
+        at += tile.shape[0]
+
     for a in range(blocks):
         here, on = slice(a * LANES, (a + 1) * LANES), slice(a * LANES, total)
         strip = dot(high[here], high[on], across, None)
         strip += dot(low[here], high[on], across, None) + dot(high[here], low[on], across, None)
-        for b in range(a, blocks):
-            out_ref[at : at + LANES, :] = strip[:, (b - a) * LANES : (b - a + 1) * LANES]
-            at += LANES
-    rounded = block_ref[...].astype(BF16)
-    proj = dot(rounded, high, across, None) + dot(rounded, low, across, None)
-    factors = proj.shape[0]
+        put(strip[:HALF, :LANES])
+        rest.append(strip[HALF:, :LANES])
+        for b in range(1, blocks - a):
+            put(strip[:, b * LANES : (b + 1) * LANES])
+    left = lax.broadcasted_iota(jnp.int32, (HALF, LANES), 1) < HALF
+    for a in range(0, blocks, 2):
+        put(jnp.where(left, pltpu.roll(rest[a], HALF, 1), rest[a + 1]))
     for b in range(blocks):
-        out_ref[at : at + factors, :] = proj[:, b * LANES : (b + 1) * LANES]
-        at += factors
+        put(proj[:, b * LANES : (b + 1) * LANES])
     if at < out_ref.shape[0]:
         out_ref[at:, :] = jnp.zeros((out_ref.shape[0] - at, LANES), F32)
 
@@ -128,15 +134,32 @@
     total = scaled_ref.shape[0]
     factors = out_ref.shape[1]
     blocks = total // LANES
+    row = lax.broadcasted_iota(jnp.int32, (LANES, LANES), 0)
+    lane = lax.broadcasted_iota(jnp.int32, (LANES, LANES), 1)
     at = 0
-    for a, b in tiles_of(total):
-        rows, columns = slice(a * LANES, (a + 1) * LANES), slice(b * LANES, (b + 1) * LANES)
-        tile = got_ref[at : at + LANES, :]
-        high_ref[rows, columns], low_ref[rows, columns] = split(tile)
-        if a != b:
-            high_ref[columns, rows], low_ref[columns, rows] = split(tile.T)
-        at += LANES
-    proj = jnp.concatenate([got_ref[at + b * factors : at + (b + 1) * factors, :] for b in range(blocks)], axis=1)
+
+    def take(rows):
+        nonlocal at
+        at += rows
+        return got_ref[at - rows : at, :]
+
+    tops = []
+    for a in range(blocks):
+        here = slice(a * LANES, (a + 1) * LANES)
+        tops.append(take(HALF))
+        for b in range(a + 1, blocks):
+            there = slice(b * LANES, (b + 1) * LANES)
+            tile = take(LANES)
+            high_ref[here, there], low_ref[here, there] = split(tile)
+            high_ref[there, here], low_ref[there, here] = split(tile.T)
+    for a in range(0, blocks, 2):
+        pair = take(HALF)
+        for c, rest in ((a, pltpu.roll(pair, HALF, 1)), (a + 1, pair)):
+            here = slice(c * LANES, (c + 1) * LANES)
+            tile = jnp.concatenate([tops[c], rest], axis=0)
+            tile = jnp.where((row >= HALF) & (lane < HALF), tile.T, tile)
+            high_ref[here, here], low_ref[here, here] = split(tile)
+    proj = jnp.concatenate([take(factors) for b in range(blocks)], axis=1)
     inward = ((1,), (0,))
     for step in range(ITERS):
         high, low = split(proj)
@@ -150,10 +173,11 @@
 
 def unpack_kernel(got_ref, out_ref):
     windows, _, width = out_ref.shape
-    parts = width // LANES
+    near, blocks = got_ref.shape[:2]
     for w in range(windows):
-        for j in range(parts):
-            out_ref[w, :, j * LANES : (j + 1) * LANES] = got_ref[w * parts + j].astype(F32)
+        for j in range(width // LANES):
+            block = w * (blocks // windows) + j // near
+            out_ref[w, :, j * LANES : (j + 1) * LANES] = got_ref[j % near, block].astype(F32)
 
 
 def on_device(returns, starts, start_block):
@@ -161,10 +185,12 @@
     factors = start_block.shape[1]
     parts = width // LANES
     rows = windows * parts
-    sides = lax.axis_size(("cols", "sub"))
+    cols, sub = lax.axis_size("cols"), lax.axis_size("sub")
+    sides = cols * sub
     total = days * rows
     assets = width * sides
-    w, j = lax.axis_index("window"), lax.axis_index("part")
+    part = ("far", "near")
+    w, j = lax.axis_index("window"), lax.axis_index(part)
     row = w * parts + j
 
     packed = pl.pallas_call(
@@ -172,14 +198,13 @@
         out_shape=jax.ShapeDtypeStruct((rows, days + EXTRA, LANES), BF16),
         in_specs=[SMEM, VMEM, VMEM],
         out_specs=VMEM,
-        compiler_params=PARAMS,
         name="pack",
     )(row[None], returns, starts)
-    got = lax.all_to_all(packed, ("window", "part"), 0, 0, tiled=True)
-
-    filled = len(tiles_of(total)) * LANES + factors * total // LANES
-    unit = 8 * sides * parts
-    height = (filled + unit - 1) // unit * unit
+    got = lax.all_to_all(packed, ("window", *part), 0, 0, tiled=True)
+
+    blocks = total // LANES
+    filled = blocks * (blocks - 1) // 2 * LANES + blocks // 2 * 3 * HALF + factors * blocks
+    height = (filled + 8 * sides - 1) // (8 * sides) * (8 * sides)
     scaled, partial = pl.pallas_call(
         gram_kernel,
         out_shape=(
@@ -196,22 +221,28 @@
         lax.dynamic_slice(start_block, (w, 0, j * LANES), (1, factors, LANES))[0],
     )
 
-    own = lax.all_to_all(partial.reshape(sides, height // sides, LANES), ("cols", "sub"), 0, 0, tiled=True)
-    own = own.sum(axis=0).reshape(parts, height // sides // parts, LANES)
-    own = lax.all_to_all(own, "part", 0, 0, tiled=True).sum(axis=0)
-    own = lax.all_to_all(jnp.broadcast_to(own[None], (parts, *own.shape)), "part", 0, 0, tiled=True)
-    whole = lax.all_gather(own.reshape(height // sides, LANES), ("cols", "sub"), tiled=True)
-
+    share = height // sides
+    padded = (share + 8 * parts - 1) // (8 * parts) * (8 * parts)
+    own = lax.all_to_all(partial.reshape(sides, share, LANES), ("sub", "cols"), 0, 0, tiled=True).sum(axis=0)
+    own = jnp.pad(own, ((0, padded - share), (0, 0))).reshape(parts, padded // parts, LANES)
+    own = lax.all_to_all(own, part, 0, 0, tiled=True).sum(axis=0)
+    own = lax.all_to_all(jnp.broadcast_to(own[None], (parts, *own.shape)), part, 0, 0, tiled=True)
+    own = own.reshape(padded, LANES)[:share]
+    own = lax.all_to_all(jnp.broadcast_to(own[None], (cols, share, LANES)), "cols", 0, 0, tiled=True)
+    whole = lax.all_gather(own.reshape(cols * share, LANES), "sub", tiled=True)
+
+    far = windows * parts // NEAR
     sent = pl.pallas_call(
         functools.partial(iterate_kernel, assets),
-        out_shape=jax.ShapeDtypeStruct((rows, factors, LANES), BF16),
+        out_shape=jax.ShapeDtypeStruct((far, factors, LANES), BF16),
         in_specs=[VMEM, VMEM],
         out_specs=VMEM,
         scratch_shapes=[pltpu.VMEM((total, total), BF16)] * 2,
         compiler_params=PARAMS,
         name="iterate",
     )(whole, scaled)
-    got = lax.all_to_all(sent, ("window", "part"), 0, 0, tiled=True)
+    got = lax.all_to_all(sent, ("window", "far"), 0, 0, tiled=True)
+    got = lax.all_to_all(jnp.broadcast_to(got[None], (NEAR, *got.shape)), "near", 0, 0, tiled=True)
     return pl.pallas_call(
         unpack_kernel,
         out_shape=jax.ShapeDtypeStruct((windows, factors, width), F32),
@@ -228,11 +259,11 @@
     def whole(returns, starts, start_block):
         windows = returns.shape[0] // groups
         split = Mesh(
-            mesh.devices.reshape(groups, windows, rows // windows, cols, sub),
-            ("groups", "window", "part", "cols", "sub"),
+            mesh.devices.reshape(groups, windows, rows // windows // NEAR, NEAR, cols, sub),
+            ("groups", "window", "far", "near", "cols", "sub"),
         )
         placed = (
-            P("groups", ("window", "part"), ("cols", "sub")),
+            P("groups", ("window", "far", "near"), ("cols", "sub")),
             P("groups", ("cols", "sub")),
             P("groups", None, ("cols", "sub")),
         )

time: 202 us -> 189 us (0.936)
  blocking collectives: 110 us -> 97.8 us
    all_gather x1, blocking collectives: 13.4 us -> 2.29 us  [on_device(): whole = lax.all_gather(own.reshape(cols * share, LANES), 'sub', tiled=True)]
    all_to_all x4 -> x6, blocking collectives: 96.4 us -> 95.5 us  [the longest x1 31.3 us: on_device(): got = lax.all_to_all(sent, ('window', 'far'), 0, 0, tiled=True)]
where the time goes in v3:
time: 189 us
  blocking collectives  97.8 us (52%)
  starting transfers between devices  45.8 us (24%)
  waiting for transfers between devices  35.6 us (19%)
  Pallas kernels  8.42 us (4%)
    all_to_all x1, starting transfers between devices, on_device(): got = lax.all_to_all(packed, ('window', *part), 0, 0, tiled=True)  45.8 us
    all_to_all x1, waiting for transfers between devices, on_device(): got = lax.all_to_all(packed, ('window', *part), 0, 0, tiled=True)  35.6 us
    all_to_all x1, blocking collectives, on_device(): got = lax.all_to_all(sent, ('window', 'far'), 0, 0, tiled=True)  31.3 us
    all_to_all x1, blocking collectives, on_device(): lax.all_to_all(partial.reshape(sides, share, LANES), ('sub', 'cols'), 0,...  15.6 us
    all_to_all x1, blocking collectives, on_device(): lax.all_to_all(jnp.broadcast_to(own[None], (parts, *own.shape)), part, 0,...  14.8 us
    all_to_all x1, blocking collectives, on_device(): own = lax.all_to_all(own, part, 0, 0, tiled=True).sum(axis=0)  14.1 us
    all_to_all x1, blocking collectives, on_device(): lax.all_to_all(jnp.broadcast_to(got[None], (NEAR, *got.shape)), 'near', 0...  10.3 us
    all_to_all x1, blocking collectives, on_device(): lax.all_to_all(jnp.broadcast_to(own[None], (cols, share, LANES)), 'cols',...  9.43 us
  transfers between devices with their start and end apart: 1, of which 1 were waited for; matrix products, arithmetic and copies ran while one was open for 0% of the time, Pallas kernels for 0%

profile of v3, /device:TPU:40, one launch (start us, length us, event | category | flops | bytes accessed | tf_op | source)
XLA Modules:
  0.0 188.5 jit_solution(5843948592880555409)
XLA Ops:
  0.0 0.0 copy-start
  0.0 1.9 pack.1
  1.9 45.8 %all-to-all-start = ((bf16[32,24,128]{2,1,0:T(8,128)(2,1)}), bf16[32,24,128]{2,1,0:T(8,128)(2,1)S(1)}, u32[]{:S(2)}, u32[]{:S(2)}) async-start(bf16[32,24,128]{2,1,0:T(8,128)(2,1)} %pack.1), calls=%async_computation | async-start | bytes 393216 | tf_op jit(solution)/shard_map/all_to_all | solution.py:203
  47.7 0.8 dynamic_slice.6.starts_ref
  48.4 0.0 copy-done
  48.4 35.6 %all-to-all-done.got_ref = bf16[32,24,128]{2,1,0:T(8,128)(2,1)S(1)} async-done(((bf16[32,24,128]{2,1,0:T(8,128)(2,1)}), bf16[32,24,128]{2,1,0:T(8,128)(2,1)S(1)}, u32[]{:S(2)}, u32[]{:S(2)}) %all-to-all-start) | async-done | bytes 196640 | tf_op jit(solution)/shard_map/all_to_all | solution.py:203
  84.0 0.8 gram.1
  84.9 15.6 %all_to_all.35 = f32[8,160,128]{2,1,0:T(8,128)S(1)} all-to-all(f32[8,160,128]{2,1,0:T(8,128)S(1)} %bitcast.7), channel_id=1, replica_groups=mesh['groups'=2,'window'=4,'far'=2,'near'=4,'cols'=4,'sub'=2] {'sub','co..., dimensions={0} | all-to-all | bytes 1310720 | tf_op jit(solution)/shard_map/all_to_all | solution.py:226
  100.5 14.1 %all_to_all.36 = f32[8,24,128]{2,1,0:T(8,128)S(1)} all-to-all(f32[8,24,128]{2,1,0:T(8,128)S(1)} %bitcast.9), channel_id=1, replica_groups=mesh['groups'=2,'window'=4,'far'=2,'near'=4,'cols'=4,'sub'=2] {'far','ne..., dimensions={0} | all-to-all | bytes 196608 | tf_op jit(solution)/shard_map/all_to_all | solution.py:228
  114.6 14.8 %all_to_all.37 = f32[8,24,128]{2,1,0:T(8,128)S(1)} all-to-all(f32[8,24,128]{2,1,0:T(8,128)S(1)} %broadcast_in_dim.9), channel_id=1, replica_groups=mesh['groups'=2,'window'=4,'far'=2,'near'=4,'cols'=4,'sub'=2] {'far','ne..., dimensions={0} | all-to-all | bytes 196608 | tf_op jit(solution)/shard_map/all_to_all | solution.py:229
  129.4 9.4 %all_to_all.38 = f32[4,160,128]{2,1,0:T(8,128)S(1)} all-to-all(f32[4,160,128]{2,1,0:T(8,128)S(1)} %broadcast_in_dim.10), channel_id=1, replica_groups=mesh['groups'=2,'window'=4,'far'=2,'near'=4,'cols'=4,'sub'=2] {'cols'}, dimensions={0} | all-to-all | bytes 655360 | tf_op jit(solution)/shard_map/all_to_all | solution.py:231
  138.8 2.3 %all_gather.3.got_ref = f32[1280,128]{1,0:T(8,128)S(1)} all-gather(f32[640,128]{1,0:T(8,128)S(1)} %bitcast.8), channel_id=1, replica_groups=mesh['groups'=2,'window'=4,'far'=2,'near'=4,'cols'=4,'sub'=2] {'sub'}, dimensions={0}, use_global_device_ids=true | all-gather | bytes 983040 | tf_op jit(solution)/shard_map/all_gather | solution.py:232
  141.1 4.9 %iterate.1 = bf16[8,32,128]{2,1,0:T(8,128)(2,1)S(1)} custom-call(f32[1280,128]{1,0:T(8,128)S(1)} %all_gather.3.got_ref, f32[512,128]{1,0:T(8,128)S(1)} %get-tuple-element.8.scaled_ref), custom_call_target="tpu_custom_call" | custom-call | tf_op jit(solution)/shard_map/iterate/pallas_call | solution.py:235
  146.0 31.3 %all_to_all.39 = bf16[8,32,128]{2,1,0:T(8,128)(2,1)S(1)} all-to-all(bf16[8,32,128]{2,1,0:T(8,128)(2,1)S(1)} %iterate.1), channel_id=1, replica_groups=mesh['groups'=2,'window'=4,'far'=2,'near'=4,'cols'=4,'sub'=2] {'window',..., dimensions={0} | all-to-all | bytes 131072 | tf_op jit(solution)/shard_map/all_to_all | solution.py:244
  177.4 10.3 %all_to_all.40.got_ref = bf16[4,8,32,128]{3,2,1,0:T(8,128)(2,1)S(1)} all-to-all(bf16[4,8,32,128]{3,2,1,0:T(8,128)(2,1)S(1)} %broadcast_in_dim.11), channel_id=1, replica_groups=mesh['groups'=2,'window'=4,'far'=2,'near'=4,'cols'=4,'sub'=2] {'near'}, dimensions={0} | all-to-all | bytes 524288 | tf_op jit(solution)/shard_map/all_to_all | solution.py:245
  187.7 0.8 unpack.1
  (8 shorter events, 0.1 us)
Async XLA Ops:
  0.0 48.4 %copy-start = (f32[4,32,1024]{2,1,0:T(8,128)S(1)}, f32[4,32,1024]{2,1,0:T(8,128)}, u32[]{:S(2)}) copy-start(f32[4,32,1024]{2,1,0:T(8,128)} %param.5) | copy-start | bytes 1572868
  1.9 82.1 %all-to-all-start = ((bf16[32,24,128]{2,1,0:T(8,128)(2,1)}), bf16[32,24,128]{2,1,0:T(8,128)(2,1)S(1)}, u32[]{:S(2)}, u32[]{:S(2)}) async-start(bf16[32,24,128]{2,1,0:T(8,128)(2,1)} %pack.1), calls=%async_computation | async-start | bytes 393216 | tf_op jit(solution)/shard_map/all_to_all | solution.py:203

commit v4 on v3

--- a/solution.py
+++ b/solution.py
@@ -12,7 +12,8 @@
 LANES = 128
 HALF = LANES // 2
 NEAR = 4
-EXTRA = 8
+EIGHT = 8
+QUAD = 4
 F32 = jnp.float32
 BF16 = jnp.bfloat16
 HIGHEST = lax.Precision.HIGHEST
@@ -39,7 +40,7 @@
     windows, days, width = returns_ref.shape
     parts = width // LANES
     day = lax.broadcasted_iota(jnp.int32, (days, width), 0) + where_ref[0] * days
-    row = lax.broadcasted_iota(jnp.int32, (EXTRA, width), 0)
+    row = lax.broadcasted_iota(jnp.int32, (QUAD, width), 0)
     for w in range(windows):
         live = day >= starts_ref[w : w + 1, :]
         kept = jnp.where(live, returns_ref[w], 0.0)
@@ -49,23 +50,32 @@
         middle = (shift - high).astype(BF16).astype(F32)
         low = (shift - high - middle).astype(BF16).astype(F32)
         shift = high + middle + low
-        rest = jnp.where(live, kept - shift, 0.0).astype(BF16)
-        carried = jnp.where(row == 0, high, jnp.where(row == 1, middle, jnp.where(row == 2, low, 0.0))).astype(BF16)
-        for j in range(parts):
-            at = slice(j * LANES, (j + 1) * LANES)
-            out_ref[w * parts + j, 0:days, :] = rest[:, at]
-            out_ref[w * parts + j, days : days + EXTRA, :] = carried[:, at]
-
-
-def gram_kernel(got_ref, starts_ref, block_ref, scaled_ref, out_ref):
-    sources, rows, _ = got_ref.shape
-    days = rows - EXTRA
+        rest = jnp.where(live, kept - shift, 0.0)
+        carried = jnp.where(row == 0, high, jnp.where(row == 1, middle, jnp.where(row == 2, low, 0.0)))
+        blocks = [rest[i : i + QUAD] for i in range(0, days, QUAD)] + [carried]
+        for i, block in enumerate(blocks):
+            block = block.astype(BF16)
+            for j in range(parts):
+                out_ref[w * parts + j, :, i * LANES : (i + 1) * LANES] = block[:, j * LANES : (j + 1) * LANES]
+
+
+def gram_kernel(where_ref, got_ref, starts_ref, block_ref, scaled_ref, out_ref):
+    sources = got_ref.shape[0]
+    days = (got_ref.shape[2] // LANES - 1) * QUAD
     total = sources * days
-    starts = starts_ref[...]
+    parts = sources // starts_ref.shape[0]
+    w = where_ref[0] // parts
+    own = pl.ds(pl.multiple_of(where_ref[0] % parts * LANES, LANES), LANES)
+    starts = starts_ref[:, own]
+    starts = jnp.sum(jnp.where(lax.broadcasted_iota(jnp.int32, starts.shape, 0) == w, starts, 0), axis=0, keepdims=True)
     got = got_ref[...].astype(F32)
-    shift = jnp.sum(got[:, days:, :], axis=1, keepdims=True)
-    values = (got[:, :days, :] + shift).reshape(total, LANES)
-    live = lax.broadcasted_iota(jnp.int32, (total, LANES), 0) >= starts
+    lanes = [got[:, :, at : at + LANES] for at in range(0, got.shape[2], LANES)]
+    shift = jnp.sum(lanes[-1], axis=1, keepdims=True)
+    eights = [jnp.concatenate(lanes[i : i + 2], axis=1) + shift for i in range(0, len(lanes) - 1, 2)]
+    values = jnp.concatenate([eight.reshape(sources * EIGHT, LANES) for eight in eights], axis=0)
+    row = lax.broadcasted_iota(jnp.int32, (total, LANES), 0)
+    eight, source = row // (sources * EIGHT), row % (sources * EIGHT) // EIGHT
+    live = source * days + eight * EIGHT + row % EIGHT >= starts
     counts = (total - starts).astype(F32)
     mean = jnp.sum(jnp.where(live, values, 0.0), axis=0, keepdims=True) / counts
     centered = jnp.where(live, values - mean, 0.0)
@@ -75,7 +85,7 @@
     high, low = split(scaled)
     blocks = total // LANES
     across = ((1,), (1,))
-    rounded = block_ref[...].astype(BF16)
+    rounded = block_ref[w, :, own].astype(BF16)
     proj = dot(rounded, high, across, None) + dot(rounded, low, across, None)
     rest = []
     at = 0
@@ -190,12 +200,11 @@
     total = days * rows
     assets = width * sides
     part = ("far", "near")
-    w, j = lax.axis_index("window"), lax.axis_index(part)
-    row = w * parts + j
+    row = lax.axis_index("window") * parts + lax.axis_index(part)
 
     packed = pl.pallas_call(
         pack_kernel,
-        out_shape=jax.ShapeDtypeStruct((rows, days + EXTRA, LANES), BF16),
+        out_shape=jax.ShapeDtypeStruct((rows, QUAD, (days // QUAD + 1) * LANES), BF16),
         in_specs=[SMEM, VMEM, VMEM],
         out_specs=VMEM,
         name="pack",
@@ -211,15 +220,11 @@
             jax.ShapeDtypeStruct((total, LANES), F32),
             jax.ShapeDtypeStruct((height, LANES), F32),
         ),
-        in_specs=[VMEM] * 3,
+        in_specs=[SMEM, VMEM, VMEM, VMEM],
         out_specs=(VMEM, VMEM),
         compiler_params=PARAMS,
         name="gram",
-    )(
-        got,
-        lax.dynamic_slice(starts, (w, j * LANES), (1, LANES)),
-        lax.dynamic_slice(start_block, (w, 0, j * LANES), (1, factors, LANES))[0],
-    )
+    )(row[None], got, starts, start_block)
 
     share = height // sides
     padded = (share + 8 * parts - 1) // (8 * parts) * (8 * parts)

time: 189 us -> 187 us (0.989)
  blocking collectives: 97.8 us -> 178 us
  starting transfers between devices: 45.8 us -> 0 us
  waiting for transfers between devices: 35.6 us -> 0 us
    all_to_all x0 -> x1, blocking collectives: none -> 79.6 us  [on_device(): got = lax.all_to_all(packed, ('window', *part), 0, 0, tiled=True)]
    all_to_all x1 -> x0, starting transfers between devices: 45.8 us -> none  [on_device(): got = lax.all_to_all(packed, ('window', *part), 0, 0, tiled=True)]
    all_to_all x1 -> x0, waiting for transfers between devices: 35.6 us -> none  [on_device(): got = lax.all_to_all(packed, ('window', *part), 0, 0, tiled=True)]
  transfers between devices with their start and end apart: 1 -> 0, of which waited for: 1 -> 0; matrix products, arithmetic and copies ran while one was open for 0% -> 0% of each run, Pallas kernels for 0% -> 0%
where the time goes in v4:
time: 187 us; the launch traced here: 186 us
  blocking collectives  178 us (95%)
  Pallas kernels  8.5 us (5%)
    all_to_all x1, blocking collectives, on_device(): got = lax.all_to_all(packed, ('window', *part), 0, 0, tiled=True)  79.6 us
    all_to_all x1, blocking collectives, on_device(): got = lax.all_to_all(sent, ('window', 'far'), 0, 0, tiled=True)  31.5 us
    all_to_all x1, blocking collectives, on_device(): lax.all_to_all(partial.reshape(sides, share, LANES), ('sub', 'cols'), 0,...  15.6 us
    all_to_all x1, blocking collectives, on_device(): lax.all_to_all(jnp.broadcast_to(own[None], (parts, *own.shape)), part, 0,...  14.8 us
    all_to_all x1, blocking collectives, on_device(): own = lax.all_to_all(own, part, 0, 0, tiled=True).sum(axis=0)  14.1 us
    all_to_all x1, blocking collectives, on_device(): lax.all_to_all(jnp.broadcast_to(got[None], (NEAR, *got.shape)), 'near', 0...  10.3 us
    all_to_all x1, blocking collectives, on_device(): lax.all_to_all(jnp.broadcast_to(own[None], (cols, share, LANES)), 'cols',...  9.43 us
    pallas_call x1, Pallas kernels, on_device(): pl.pallas_call(functools.partial(iterate_kernel, assets), out_shape=jax.S...  4.88 us

profile of v4, /device:TPU:40, one launch (start us, length us, event | category | flops | bytes accessed | tf_op | source)
XLA Modules:
  0.0 186.2 jit_solution(10496077289108048334)
XLA Ops:
  0.0 0.0 copy-start
  0.0 1.9 %pack.1 = bf16[32,4,640]{2,1,0:T(4,128)(2,1)} custom-call(s32[1]{0:T(128)} %bitcast.where_ref, f32[4,16,1024]{2,1,0:T(8,128)} %returns_ref.1, s32[4,1024]{1,0:T(4,128)} %starts_ref.3), custom_call_target="tpu_custom_call" | custom-call | tf_op jit(solution)/shard_map/pack/pallas_call | solution.py:205
  1.9 0.0 copy-start.1
  1.9 79.6 %all_to_all.35.got_ref = bf16[32,4,640]{2,1,0:T(4,128)(2,1)S(1)} all-to-all(bf16[32,4,640]{2,1,0:T(4,128)(2,1)} %pack.1), channel_id=1, replica_groups=mesh['groups'=2,'window'=4,'far'=2,'near'=4,'cols'=4,'sub'=2] {'window',..., dimensions={0} | all-to-all | bytes 327680 | tf_op jit(solution)/shard_map/all_to_all | solution.py:212
  81.5 0.0 copy-done
  81.5 0.0 copy-done.1
  81.5 0.9 gram.1
  82.4 15.6 %all_to_all.36 = f32[8,160,128]{2,1,0:T(8,128)S(1)} all-to-all(f32[8,160,128]{2,1,0:T(8,128)S(1)} %bitcast.5), channel_id=1, replica_groups=mesh['groups'=2,'window'=4,'far'=2,'near'=4,'cols'=4,'sub'=2] {'sub','co..., dimensions={0} | all-to-all | bytes 1310720 | tf_op jit(solution)/shard_map/all_to_all | solution.py:231
  98.0 14.1 %all_to_all.37 = f32[8,24,128]{2,1,0:T(8,128)S(1)} all-to-all(f32[8,24,128]{2,1,0:T(8,128)S(1)} %bitcast.7), channel_id=1, replica_groups=mesh['groups'=2,'window'=4,'far'=2,'near'=4,'cols'=4,'sub'=2] {'far','ne..., dimensions={0} | all-to-all | bytes 196608 | tf_op jit(solution)/shard_map/all_to_all | solution.py:233
  112.1 14.8 %all_to_all.38 = f32[8,24,128]{2,1,0:T(8,128)S(1)} all-to-all(f32[8,24,128]{2,1,0:T(8,128)S(1)} %broadcast_in_dim.9), channel_id=1, replica_groups=mesh['groups'=2,'window'=4,'far'=2,'near'=4,'cols'=4,'sub'=2] {'far','ne..., dimensions={0} | all-to-all | bytes 196608 | tf_op jit(solution)/shard_map/all_to_all | solution.py:234
  126.9 9.4 %all_to_all.39 = f32[4,160,128]{2,1,0:T(8,128)S(1)} all-to-all(f32[4,160,128]{2,1,0:T(8,128)S(1)} %broadcast_in_dim.10), channel_id=1, replica_groups=mesh['groups'=2,'window'=4,'far'=2,'near'=4,'cols'=4,'sub'=2] {'cols'}, dimensions={0} | all-to-all | bytes 655360 | tf_op jit(solution)/shard_map/all_to_all | solution.py:236
  136.4 2.3 %all_gather.3.got_ref = f32[1280,128]{1,0:T(8,128)S(1)} all-gather(f32[640,128]{1,0:T(8,128)S(1)} %bitcast.6), channel_id=1, replica_groups=mesh['groups'=2,'window'=4,'far'=2,'near'=4,'cols'=4,'sub'=2] {'sub'}, dimensions={0}, use_global_device_ids=true | all-gather | bytes 983040 | tf_op jit(solution)/shard_map/all_gather | solution.py:237
  138.7 4.9 %iterate.1 = bf16[8,32,128]{2,1,0:T(8,128)(2,1)S(1)} custom-call(f32[1280,128]{1,0:T(8,128)S(1)} %all_gather.3.got_ref, f32[512,128]{1,0:T(8,128)S(1)} %get-tuple-element.8.scaled_ref), custom_call_target="tpu_custom_call" | custom-call | tf_op jit(solution)/shard_map/iterate/pallas_call | solution.py:240
  143.6 31.5 %all_to_all.40 = bf16[8,32,128]{2,1,0:T(8,128)(2,1)S(1)} all-to-all(bf16[8,32,128]{2,1,0:T(8,128)(2,1)S(1)} %iterate.1), channel_id=1, replica_groups=mesh['groups'=2,'window'=4,'far'=2,'near'=4,'cols'=4,'sub'=2] {'window',..., dimensions={0} | all-to-all | bytes 131072 | tf_op jit(solution)/shard_map/all_to_all | solution.py:249
  175.1 10.3 %all_to_all.41.got_ref = bf16[4,8,32,128]{3,2,1,0:T(8,128)(2,1)S(1)} all-to-all(bf16[4,8,32,128]{3,2,1,0:T(8,128)(2,1)S(1)} %broadcast_in_dim.11), channel_id=1, replica_groups=mesh['groups'=2,'window'=4,'far'=2,'near'=4,'cols'=4,'sub'=2] {'near'}, dimensions={0} | all-to-all | bytes 524288 | tf_op jit(solution)/shard_map/all_to_all | solution.py:250
  185.4 0.8 unpack.1
  (7 shorter events, 0.1 us)
Async XLA Ops:
  0.0 81.5 %copy-start = (f32[4,32,1024]{2,1,0:T(8,128)S(1)}, f32[4,32,1024]{2,1,0:T(8,128)}, u32[]{:S(2)}) copy-start(f32[4,32,1024]{2,1,0:T(8,128)} %block_ref.1) | copy-start | bytes 1572868
  1.9 79.6 %copy-start.1 = (s32[4,1024]{1,0:T(4,128)S(1)}, s32[4,1024]{1,0:T(4,128)}, u32[]{:S(2)}) copy-start(s32[4,1024]{1,0:T(4,128)} %starts_ref.3) | copy-start | bytes 49156

commit v5 on v4

--- a/solution.py
+++ b/solution.py
@@ -59,7 +59,7 @@
                 out_ref[w * parts + j, :, i * LANES : (i + 1) * LANES] = block[:, j * LANES : (j + 1) * LANES]
 
 
-def gram_kernel(where_ref, got_ref, starts_ref, block_ref, scaled_ref, out_ref):
+def scale_kernel(where_ref, got_ref, starts_ref, block_ref, out_ref):
     sources = got_ref.shape[0]
     days = (got_ref.shape[2] // LANES - 1) * QUAD
     total = sources * days
@@ -81,18 +81,25 @@
     centered = jnp.where(live, values - mean, 0.0)
     squares = jnp.sum(centered * centered, axis=0, keepdims=True)
     scaled = centered * lax.rsqrt(squares + 1.0)
-    scaled_ref[...] = scaled
-    high, low = split(scaled)
+    out_ref[0:total, :] = scaled
+    out_ref[total:, :] = block_ref[w, :, own].astype(BF16).astype(F32)
+
+
+def gram_kernel(where_ref, both_ref, out_ref, all_ref):
+    cores, rows, _ = both_ref.shape
+    total = rows // LANES * LANES
+    both = jnp.concatenate([both_ref[c] for c in range(cores)], axis=1)
+    high, low = split(both[:total])
+    rounded = both[total:].astype(BF16)
     blocks = total // LANES
     across = ((1,), (1,))
-    rounded = block_ref[w, :, own].astype(BF16)
     proj = dot(rounded, high, across, None) + dot(rounded, low, across, None)
     rest = []
     at = 0
 
     def put(tile):
         nonlocal at
-        out_ref[at : at + tile.shape[0], :] = tile
+        all_ref[at : at + tile.shape[0], :] = tile
         at += tile.shape[0]
 
     for a in range(blocks):
@@ -108,8 +115,10 @@
         put(jnp.where(left, pltpu.roll(rest[a], HALF, 1), rest[a + 1]))
     for b in range(blocks):
         put(proj[:, b * LANES : (b + 1) * LANES])
-    if at < out_ref.shape[0]:
-        out_ref[at:, :] = jnp.zeros((out_ref.shape[0] - at, LANES), F32)
+    if at < all_ref.shape[0]:
+        all_ref[at:, :] = jnp.zeros((all_ref.shape[0] - at, LANES), F32)
+    share = out_ref.shape[0]
+    out_ref[...] = all_ref[pl.ds(pl.multiple_of(where_ref[0] * share, EIGHT), share), :]
 
 
 def inverse_lower(gram):
@@ -141,8 +150,8 @@
 
 
 def iterate_kernel(assets, got_ref, scaled_ref, out_ref, high_ref, low_ref):
-    total = scaled_ref.shape[0]
     factors = out_ref.shape[1]
+    total = scaled_ref.shape[0] - factors
     blocks = total // LANES
     row = lax.broadcasted_iota(jnp.int32, (LANES, LANES), 0)
     lane = lax.broadcasted_iota(jnp.int32, (LANES, LANES), 1)
@@ -177,7 +186,7 @@
         moved = stacked[:factors] + (stacked[factors:] + dot(high, low_ref[...], inward, None))
         gram = dot(moved, proj, ((1,), (1,))) * (1.0 / assets)
         proj = dot(inverse_lower(gram), moved if step < ITERS - 1 else proj, inward)
-    loadings = dot3(proj, scaled_ref[...], inward).astype(BF16)
+    loadings = dot3(proj, scaled_ref[0:total, :], inward).astype(BF16)
     out_ref[...] = jnp.broadcast_to(loadings[None], out_ref.shape)
 
 
@@ -214,25 +223,29 @@
     blocks = total // LANES
     filled = blocks * (blocks - 1) // 2 * LANES + blocks // 2 * 3 * HALF + factors * blocks
     height = (filled + 8 * sides - 1) // (8 * sides) * (8 * sides)
-    scaled, partial = pl.pallas_call(
+    scaled = pl.pallas_call(
+        scale_kernel,
+        out_shape=jax.ShapeDtypeStruct((total + factors, LANES), F32),
+        in_specs=[SMEM, VMEM, VMEM, VMEM],
+        out_specs=VMEM,
+        compiler_params=PARAMS,
+        name="scale",
+    )(row[None], got, starts, start_block)
+    both = lax.all_gather(scaled, "sub")
+    partial = pl.pallas_call(
         gram_kernel,
-        out_shape=(
-            jax.ShapeDtypeStruct((total, LANES), F32),
-            jax.ShapeDtypeStruct((height, LANES), F32),
-        ),
-        in_specs=[SMEM, VMEM, VMEM, VMEM],
-        out_specs=(VMEM, VMEM),
+        out_shape=jax.ShapeDtypeStruct((height // sub, LANES), F32),
+        in_specs=[SMEM, VMEM],
+        out_specs=VMEM,
+        scratch_shapes=[pltpu.VMEM((height, LANES), F32)],
         compiler_params=PARAMS,
         name="gram",
-    )(row[None], got, starts, start_block)
+    )(lax.axis_index("sub")[None], both)
 
     share = height // sides
-    padded = (share + 8 * parts - 1) // (8 * parts) * (8 * parts)
-    own = lax.all_to_all(partial.reshape(sides, share, LANES), ("sub", "cols"), 0, 0, tiled=True).sum(axis=0)
-    own = jnp.pad(own, ((0, padded - share), (0, 0))).reshape(parts, padded // parts, LANES)
-    own = lax.all_to_all(own, part, 0, 0, tiled=True).sum(axis=0)
-    own = lax.all_to_all(jnp.broadcast_to(own[None], (parts, *own.shape)), part, 0, 0, tiled=True)
-    own = own.reshape(padded, LANES)[:share]
+    own = lax.all_to_all(partial.reshape(cols, share, LANES), "cols", 0, 0, tiled=True).sum(axis=0)
+    own = lax.all_to_all(jnp.broadcast_to(own[None], (NEAR, share, LANES)), "near", 0, 0, tiled=True).sum(axis=0)
+    own = lax.all_gather(own, "far").sum(axis=0)
     own = lax.all_to_all(jnp.broadcast_to(own[None], (cols, share, LANES)), "cols", 0, 0, tiled=True)
     whole = lax.all_gather(own.reshape(cols * share, LANES), "sub", tiled=True)
 

time: 187 us -> 176 us (0.941)
  blocking collectives: 178 us -> 87.4 us
  starting transfers between devices: 0 us -> 45.9 us
  waiting for transfers between devices: 0 us -> 33.7 us
    all_to_all x4 -> x2, blocking collectives: 124 us -> 24.2 us  [the longest x1 12.1 us: on_device(): lax.all_to_all(jnp.broadcast_to(own[None], (NEAR, share, LANES)), 'near',...]
    all_to_all x0 -> x1, starting transfers between devices: none -> 45.9 us  [on_device(): got = lax.all_to_all(packed, ('window', *part), 0, 0, tiled=True)]
    all_to_all x0 -> x1, waiting for transfers between devices: none -> 33.7 us  [on_device(): got = lax.all_to_all(packed, ('window', *part), 0, 0, tiled=True)]
    all_gather x0 -> x2, blocking collectives: none -> 13.9 us  [the longest x1 11.7 us: on_device(): own = lax.all_gather(own, 'far').sum(axis=0)]
    all_to_all x1, blocking collectives: 31.5 us -> 26.2 us  [on_device(): got = lax.all_to_all(sent, ('window', 'far'), 0, 0, tiled=True)]
  transfers between devices with their start and end apart: 0 -> 1, of which waited for: 0 -> 1; matrix products, arithmetic and copies ran while one was open for 0% -> 0% of each run, Pallas kernels for 0% -> 0%
where the time goes in v5:
time: 176 us
  blocking collectives  87.4 us (50%)
  starting transfers between devices  45.9 us (26%)
  waiting for transfers between devices  33.7 us (19%)
  Pallas kernels  8.84 us (5%)
    all_to_all x1, starting transfers between devices, on_device(): got = lax.all_to_all(packed, ('window', *part), 0, 0, tiled=True)  45.9 us
    all_to_all x1, waiting for transfers between devices, on_device(): got = lax.all_to_all(packed, ('window', *part), 0, 0, tiled=True)  33.7 us
    all_to_all x1, blocking collectives, on_device(): got = lax.all_to_all(sent, ('window', 'far'), 0, 0, tiled=True)  26.2 us
    all_to_all x1, blocking collectives, on_device(): lax.all_to_all(jnp.broadcast_to(own[None], (NEAR, share, LANES)), 'near',...  12.1 us
    all_to_all x1, blocking collectives, on_device(): lax.all_to_all(partial.reshape(cols, share, LANES), 'cols', 0, 0, tiled=T...  12.1 us
    all_gather x1, blocking collectives, on_device(): own = lax.all_gather(own, 'far').sum(axis=0)  11.7 us
    all_to_all x1, blocking collectives, on_device(): lax.all_to_all(jnp.broadcast_to(got[None], (NEAR, *got.shape)), 'near', 0...  11.2 us
    all_to_all x1, blocking collectives, on_device(): lax.all_to_all(jnp.broadcast_to(own[None], (cols, share, LANES)), 'cols',...  9.56 us
  transfers between devices with their start and end apart: 1, of which 1 were waited for; matrix products, arithmetic and copies ran while one was open for 0% of the time, Pallas kernels for 0%

profile of v5, /device:TPU:40, one launch (start us, length us, event | category | flops | bytes accessed | tf_op | source)
XLA Modules:
  0.0 176.0 jit_solution(3529663319085443298)
XLA Ops:
  0.0 0.0 copy-start
  0.0 1.9 %pack.1 = bf16[32,4,640]{2,1,0:T(4,128)(2,1)} custom-call(s32[1]{0:T(128)} %bitcast.1.where_ref, f32[4,16,1024]{2,1,0:T(8,128)} %returns_ref.1, s32[4,1024]{1,0:T(4,128)} %starts_ref.3), custom_call_target="tpu_custom_call" | custom-call | tf_op jit(solution)/shard_map/pack/pallas_call | solution.py:214
  1.9 0.0 copy-start.1
  1.9 45.9 %all-to-all-start = ((bf16[32,4,640]{2,1,0:T(4,128)(2,1)}), bf16[32,4,640]{2,1,0:T(4,128)(2,1)S(1)}, u32[]{:S(2)}, u32[]{:S(2)}) async-start(bf16[32,4,640]{2,1,0:T(4,128)(2,1)} %pack.1), calls=%async_computation | async-start | bytes 327680 | tf_op jit(solution)/shard_map/all_to_all | solution.py:221
  47.8 33.7 %all-to-all-done.got_ref = bf16[32,4,640]{2,1,0:T(4,128)(2,1)S(1)} async-done(((bf16[32,4,640]{2,1,0:T(4,128)(2,1)}), bf16[32,4,640]{2,1,0:T(4,128)(2,1)S(1)}, u32[]{:S(2)}, u32[]{:S(2)}) %all-to-all-start) | async-done | bytes 163872 | tf_op jit(solution)/shard_map/all_to_all | solution.py:221
  81.5 0.0 copy-done
  81.5 0.0 copy-done.1
  81.5 0.3 scale.1.scaled_ref
  81.8 2.3 %all-gather = f32[1088,128]{1,0:T(8,128)S(1)} all-gather(f32[544,128]{1,0:T(8,128)S(1)} %scale.1.scaled_ref), channel_id=2, replica_groups=mesh['groups'=2,'window'=4,'far'=2,'near'=4,'cols'=4,'sub'=2] {'sub'}, dimensions={0}, use_global_device_ids=true | all-gather | bytes 835584 | tf_op jit(solution)/shard_map/all_gather | solution.py:234
  84.1 0.9 gram.1
  85.0 12.1 %all_to_all.30 = f32[4,160,128]{2,1,0:T(8,128)S(1)} all-to-all(f32[4,160,128]{2,1,0:T(8,128)S(1)} %bitcast.7), channel_id=1, replica_groups=mesh['groups'=2,'window'=4,'far'=2,'near'=4,'cols'=4,'sub'=2] {'cols'}, dimensions={0} | all-to-all | bytes 655360 | tf_op jit(solution)/shard_map/all_to_all | solution.py:246
  97.1 12.1 %all_to_all.31 = f32[4,160,128]{2,1,0:T(8,128)S(1)} all-to-all(f32[4,160,128]{2,1,0:T(8,128)S(1)} %broadcast_in_dim.12), channel_id=1, replica_groups=mesh['groups'=2,'window'=4,'far'=2,'near'=4,'cols'=4,'sub'=2] {'near'}, dimensions={0} | all-to-all | bytes 655360 | tf_op jit(solution)/shard_map/all_to_all | solution.py:247
  109.3 11.7 %all-gather.1 = f32[320,128]{1,0:T(8,128)S(1)} all-gather(f32[160,128]{1,0:T(8,128)S(1)} %reduce_sum.28), channel_id=3, replica_groups=mesh['groups'=2,'window'=4,'far'=2,'near'=4,'cols'=4,'sub'=2] {'far'}, dimensions={0}, use_global_device_ids=true | all-gather | bytes 245760 | tf_op jit(solution)/shard_map/all_gather | solution.py:248
  121.0 9.6 %all_to_all.32 = f32[4,160,128]{2,1,0:T(8,128)S(1)} all-to-all(f32[4,160,128]{2,1,0:T(8,128)S(1)} %broadcast_in_dim.13), channel_id=1, replica_groups=mesh['groups'=2,'window'=4,'far'=2,'near'=4,'cols'=4,'sub'=2] {'cols'}, dimensions={0} | all-to-all | bytes 655360 | tf_op jit(solution)/shard_map/all_to_all | solution.py:249
  130.6 2.3 %all_gather.19.got_ref = f32[1280,128]{1,0:T(8,128)S(1)} all-gather(f32[640,128]{1,0:T(8,128)S(1)} %bitcast.8), channel_id=1, replica_groups=mesh['groups'=2,'window'=4,'far'=2,'near'=4,'cols'=4,'sub'=2] {'sub'}, dimensions={0}, use_global_device_ids=true | all-gather | bytes 983040 | tf_op jit(solution)/shard_map/all_gather | solution.py:250
  132.9 4.9 %iterate.1 = bf16[8,32,128]{2,1,0:T(8,128)(2,1)S(1)} custom-call(f32[1280,128]{1,0:T(8,128)S(1)} %all_gather.19.got_ref, f32[544,128]{1,0:T(8,128)S(1)} %scale.1.scaled_ref), custom_call_target="tpu_custom_call" | custom-call | tf_op jit(solution)/shard_map/iterate/pallas_call | solution.py:253
  137.7 26.2 %all_to_all.33 = bf16[8,32,128]{2,1,0:T(8,128)(2,1)S(1)} all-to-all(bf16[8,32,128]{2,1,0:T(8,128)(2,1)S(1)} %iterate.1), channel_id=1, replica_groups=mesh['groups'=2,'window'=4,'far'=2,'near'=4,'cols'=4,'sub'=2] {'window',..., dimensions={0} | all-to-all | bytes 131072 | tf_op jit(solution)/shard_map/all_to_all | solution.py:262
  164.0 11.2 %all_to_all.34.got_ref = bf16[4,8,32,128]{3,2,1,0:T(8,128)(2,1)S(1)} all-to-all(bf16[4,8,32,128]{3,2,1,0:T(8,128)(2,1)S(1)} %broadcast_in_dim.14), channel_id=1, replica_groups=mesh['groups'=2,'window'=4,'far'=2,'near'=4,'cols'=4,'sub'=2] {'near'}, dimensions={0} | all-to-all | bytes 524288 | tf_op jit(solution)/shard_map/all_to_all | solution.py:263
  175.2 0.8 unpack.1
  (6 shorter events, 0.1 us)
Async XLA Ops:
  0.0 81.5 %copy-start = (f32[4,32,1024]{2,1,0:T(8,128)S(1)}, f32[4,32,1024]{2,1,0:T(8,128)}, u32[]{:S(2)}) copy-start(f32[4,32,1024]{2,1,0:T(8,128)} %block_ref.1) | copy-start | bytes 1572868
  1.9 79.6 %copy-start.1 = (s32[4,1024]{1,0:T(4,128)S(1)}, s32[4,1024]{1,0:T(4,128)}, u32[]{:S(2)}) copy-start(s32[4,1024]{1,0:T(4,128)} %starts_ref.3) | copy-start | bytes 49156
  1.9 79.6 %all-to-all-start = ((bf16[32,4,640]{2,1,0:T(4,128)(2,1)}), bf16[32,4,640]{2,1,0:T(4,128)(2,1)S(1)}, u32[]{:S(2)}, u32[]{:S(2)}) async-start(bf16[32,4,640]{2,1,0:T(4,128)(2,1)} %pack.1), calls=%async_computation | async-start | bytes 327680 | tf_op jit(solution)/shard_map/all_to_all | solution.py:221

commit v6 on v5

--- a/solution.py
+++ b/solution.py
@@ -208,7 +208,7 @@
     sides = cols * sub
     total = days * rows
     assets = width * sides
-    part = ("far", "near")
+    part, quad, block = ("far", "mid", "near"), ("mid", "near"), ("near", "cols")
     row = lax.axis_index("window") * parts + lax.axis_index(part)
 
     packed = pl.pallas_call(
@@ -222,7 +222,8 @@
 
     blocks = total // LANES
     filled = blocks * (blocks - 1) // 2 * LANES + blocks // 2 * 3 * HALF + factors * blocks
-    height = (filled + 8 * sides - 1) // (8 * sides) * (8 * sides)
+    unit = EIGHT * sub * lax.axis_size(block)
+    height = (filled + unit - 1) // unit * unit
     scaled = pl.pallas_call(
         scale_kernel,
         out_shape=jax.ShapeDtypeStruct((total + factors, LANES), F32),
@@ -242,12 +243,13 @@
         name="gram",
     )(lax.axis_index("sub")[None], both)
 
-    share = height // sides
-    own = lax.all_to_all(partial.reshape(cols, share, LANES), "cols", 0, 0, tiled=True).sum(axis=0)
-    own = lax.all_to_all(jnp.broadcast_to(own[None], (NEAR, share, LANES)), "near", 0, 0, tiled=True).sum(axis=0)
+    pieces = lax.axis_size(block)
+    share = height // sub // pieces
+    own = lax.all_to_all(partial.reshape(pieces, share, LANES), block, 0, 0, tiled=True).sum(axis=0)
+    own = lax.all_gather(own, "mid").sum(axis=0)
     own = lax.all_gather(own, "far").sum(axis=0)
-    own = lax.all_to_all(jnp.broadcast_to(own[None], (cols, share, LANES)), "cols", 0, 0, tiled=True)
-    whole = lax.all_gather(own.reshape(cols * share, LANES), "sub", tiled=True)
+    own = lax.all_to_all(jnp.broadcast_to(own[None], (pieces, share, LANES)), block, 0, 0, tiled=True)
+    whole = lax.all_gather(own.reshape(height // sub, LANES), "sub", tiled=True)
 
     far = windows * parts // NEAR
     sent = pl.pallas_call(
@@ -260,7 +262,7 @@
         name="iterate",
     )(whole, scaled)
     got = lax.all_to_all(sent, ("window", "far"), 0, 0, tiled=True)
-    got = lax.all_to_all(jnp.broadcast_to(got[None], (NEAR, *got.shape)), "near", 0, 0, tiled=True)
+    got = lax.all_to_all(jnp.broadcast_to(got[None], (NEAR, *got.shape)), quad, 0, 0, tiled=True)
     return pl.pallas_call(
         unpack_kernel,
         out_shape=jax.ShapeDtypeStruct((windows, factors, width), F32),
@@ -277,11 +279,11 @@
     def whole(returns, starts, start_block):
         windows = returns.shape[0] // groups
         split = Mesh(
-            mesh.devices.reshape(groups, windows, rows // windows // NEAR, NEAR, cols, sub),
-            ("groups", "window", "far", "near", "cols", "sub"),
+            mesh.devices.reshape(groups, windows, rows // windows // NEAR, NEAR // 2, 2, cols, sub),
+            ("groups", "window", "far", "mid", "near", "cols", "sub"),
         )
         placed = (
-            P("groups", ("window", "far", "near"), ("cols", "sub")),
+            P("groups", ("window", "far", "mid", "near"), ("cols", "sub")),
             P("groups", ("cols", "sub")),
             P("groups", None, ("cols", "sub")),
         )

time: 176 us -> 170 us (0.966)
  blocking collectives: 87.4 us -> 80.8 us
    all_to_all x4 -> x3, blocking collectives: 44.9 us -> 33.2 us  [the longest x1 12.8 us: on_device(): lax.all_to_all(partial.reshape(pieces, share, LANES), block, 0, 0, tiled=...]
    all_gather x1 -> x2, blocking collectives: 2.29 us -> 8.34 us  [the longest x1 6.04 us: on_device(): own = lax.all_gather(own, 'mid').sum(axis=0)]
    all_gather x1, blocking collectives: 11.7 us -> 9.3 us  [on_device(): own = lax.all_gather(own, 'far').sum(axis=0)]
where the time goes in v6:
time: 170 us; the launch traced here: 169 us
  blocking collectives  80.8 us (48%)
  starting transfers between devices  45.9 us (27%)
  waiting for transfers between devices  33.7 us (20%)
  Pallas kernels  8.84 us (5%)
    all_to_all x1, starting transfers between devices, on_device(): got = lax.all_to_all(packed, ('window', *part), 0, 0, tiled=True)  45.9 us
    all_to_all x1, waiting for transfers between devices, on_device(): got = lax.all_to_all(packed, ('window', *part), 0, 0, tiled=True)  33.7 us
    all_to_all x1, blocking collectives, on_device(): got = lax.all_to_all(sent, ('window', 'far'), 0, 0, tiled=True)  27.7 us
    all_to_all x1, blocking collectives, on_device(): lax.all_to_all(partial.reshape(pieces, share, LANES), block, 0, 0, tiled=...  12.8 us
    all_to_all x1, blocking collectives, on_device(): lax.all_to_all(jnp.broadcast_to(own[None], (pieces, share, LANES)), block...  10.2 us
    all_to_all x1, blocking collectives, on_device(): lax.all_to_all(jnp.broadcast_to(got[None], (NEAR, *got.shape)), quad, 0,...  10.2 us
    all_gather x1, blocking collectives, on_device(): own = lax.all_gather(own, 'far').sum(axis=0)  9.3 us
    all_gather x1, blocking collectives, on_device(): own = lax.all_gather(own, 'mid').sum(axis=0)  6.04 us
  transfers between devices with their start and end apart: 1, of which 1 were waited for; matrix products, arithmetic and copies ran while one was open for 0% of the time, Pallas kernels for 0%

profile of v6, /device:TPU:40, one launch (start us, length us, event | category | flops | bytes accessed | tf_op | source)
XLA Modules:
  0.0 169.4 jit_solution(1957222424575240605)
XLA Ops:
  0.0 0.0 copy-start
  0.0 1.9 %pack.1 = bf16[32,4,640]{2,1,0:T(4,128)(2,1)} custom-call(s32[1]{0:T(128)} %bitcast.1.where_ref, f32[4,16,1024]{2,1,0:T(8,128)} %returns_ref.1, s32[4,1024]{1,0:T(4,128)} %starts_ref.3), custom_call_target="tpu_custom_call" | custom-call | tf_op jit(solution)/shard_map/pack/pallas_call | solution.py:214
  1.9 0.0 copy-start.1
  1.9 45.9 %all-to-all-start = ((bf16[32,4,640]{2,1,0:T(4,128)(2,1)}), bf16[32,4,640]{2,1,0:T(4,128)(2,1)S(1)}, u32[]{:S(2)}, u32[]{:S(2)}) async-start(bf16[32,4,640]{2,1,0:T(4,128)(2,1)} %pack.1), calls=%async_computation | async-start | bytes 327680 | tf_op jit(solution)/shard_map/all_to_all | solution.py:221
  47.8 33.7 %all-to-all-done.got_ref = bf16[32,4,640]{2,1,0:T(4,128)(2,1)S(1)} async-done(((bf16[32,4,640]{2,1,0:T(4,128)(2,1)}), bf16[32,4,640]{2,1,0:T(4,128)(2,1)S(1)}, u32[]{:S(2)}, u32[]{:S(2)}) %all-to-all-start) | async-done | bytes 163872 | tf_op jit(solution)/shard_map/all_to_all | solution.py:221
  81.5 0.0 copy-done
  81.5 0.0 copy-done.1
  81.5 0.3 scale.1.scaled_ref
  81.8 2.3 %all-gather = f32[1088,128]{1,0:T(8,128)S(1)} all-gather(f32[544,128]{1,0:T(8,128)S(1)} %scale.1.scaled_ref), channel_id=2, replica_groups=mesh['groups'=2,'window'=4,'far'=2,'mid'=2,'near'=2,'cols'=4,'sub'=2] {'..., dimensions={0}, use_global_device_ids=true | all-gather | bytes 835584 | tf_op jit(solution)/shard_map/all_gather | solution.py:235
  84.1 0.9 gram.1
  85.0 12.8 %all_to_all.25 = f32[8,80,128]{2,1,0:T(8,128)S(1)} all-to-all(f32[8,80,128]{2,1,0:T(8,128)S(1)} %bitcast.8), channel_id=1, replica_groups=mesh['groups'=2,'window'=4,'far'=2,'mid'=2,'near'=2,'cols'=4,'sub'=2] {'..., dimensions={0} | all-to-all | bytes 655360 | tf_op jit(solution)/shard_map/all_to_all | solution.py:248
  97.8 6.0 %all-gather.1 = f32[160,128]{1,0:T(8,128)S(1)} all-gather(f32[80,128]{1,0:T(8,128)S(1)} %reduce_sum.27), channel_id=3, replica_groups=mesh['groups'=2,'window'=4,'far'=2,'mid'=2,'near'=2,'cols'=4,'sub'=2] {'..., dimensions={0}, use_global_device_ids=true | all-gather | bytes 122880 | tf_op jit(solution)/shard_map/all_gather | solution.py:249
  103.9 9.3 %all-gather.2 = f32[160,128]{1,0:T(8,128)S(1)} all-gather(f32[80,128]{1,0:T(8,128)S(1)} %reduce_sum.28), channel_id=4, replica_groups=mesh['groups'=2,'window'=4,'far'=2,'mid'=2,'near'=2,'cols'=4,'sub'=2] {'..., dimensions={0}, use_global_device_ids=true | all-gather | bytes 122880 | tf_op jit(solution)/shard_map/all_gather | solution.py:250
  113.2 10.2 %all_to_all.26 = f32[8,80,128]{2,1,0:T(8,128)S(1)} all-to-all(f32[8,80,128]{2,1,0:T(8,128)S(1)} %broadcast_in_dim.10), channel_id=1, replica_groups=mesh['groups'=2,'window'=4,'far'=2,'mid'=2,'near'=2,'cols'=4,'sub'=2] {'..., dimensions={0} | all-to-all | bytes 655360 | tf_op jit(solution)/shard_map/all_to_all | solution.py:251
  123.4 2.3 %all_gather.27.got_ref = f32[1280,128]{1,0:T(8,128)S(1)} all-gather(f32[640,128]{1,0:T(8,128)S(1)} %bitcast.9), channel_id=1, replica_groups=mesh['groups'=2,'window'=4,'far'=2,'mid'=2,'near'=2,'cols'=4,'sub'=2] {'..., dimensions={0}, use_global_device_ids=true | all-gather | bytes 983040 | tf_op jit(solution)/shard_map/all_gather | solution.py:252
  125.7 4.9 %iterate.1 = bf16[8,32,128]{2,1,0:T(8,128)(2,1)S(1)} custom-call(f32[1280,128]{1,0:T(8,128)S(1)} %all_gather.27.got_ref, f32[544,128]{1,0:T(8,128)S(1)} %scale.1.scaled_ref), custom_call_target="tpu_custom_call" | custom-call | tf_op jit(solution)/shard_map/iterate/pallas_call | solution.py:255
  130.6 27.7 %all_to_all.27 = bf16[8,32,128]{2,1,0:T(8,128)(2,1)S(1)} all-to-all(bf16[8,32,128]{2,1,0:T(8,128)(2,1)S(1)} %iterate.1), channel_id=1, replica_groups=mesh['groups'=2,'window'=4,'far'=2,'mid'=2,'near'=2,'cols'=4,'sub'=2] {'..., dimensions={0} | all-to-all | bytes 131072 | tf_op jit(solution)/shard_map/all_to_all | solution.py:264
  158.4 10.2 %all_to_all.28.got_ref = bf16[4,8,32,128]{3,2,1,0:T(8,128)(2,1)S(1)} all-to-all(bf16[4,8,32,128]{3,2,1,0:T(8,128)(2,1)S(1)} %broadcast_in_dim.22), channel_id=1, replica_groups=mesh['groups'=2,'window'=4,'far'=2,'mid'=2,'near'=2,'cols'=4,'sub'=2] {'..., dimensions={0} | all-to-all | bytes 524288 | tf_op jit(solution)/shard_map/all_to_all | solution.py:265
  168.6 0.8 unpack.1
  (5 shorter events, 0.1 us)
Async XLA Ops:
  0.0 81.5 %copy-start = (f32[4,32,1024]{2,1,0:T(8,128)S(1)}, f32[4,32,1024]{2,1,0:T(8,128)}, u32[]{:S(2)}) copy-start(f32[4,32,1024]{2,1,0:T(8,128)} %block_ref.1) | copy-start | bytes 1572868
  1.9 79.6 %copy-start.1 = (s32[4,1024]{1,0:T(4,128)S(1)}, s32[4,1024]{1,0:T(4,128)}, u32[]{:S(2)}) copy-start(s32[4,1024]{1,0:T(4,128)} %starts_ref.3) | copy-start | bytes 49156
  1.9 79.6 %all-to-all-start = ((bf16[32,4,640]{2,1,0:T(4,128)(2,1)}), bf16[32,4,640]{2,1,0:T(4,128)(2,1)S(1)}, u32[]{:S(2)}, u32[]{:S(2)}) async-start(bf16[32,4,640]{2,1,0:T(4,128)(2,1)} %pack.1), calls=%async_computation | async-start | bytes 327680 | tf_op jit(solution)/shard_map/all_to_all | solution.py:221

commit v7 on v6

--- a/solution.py
+++ b/solution.py
@@ -18,6 +18,7 @@
 BF16 = jnp.bfloat16
 HIGHEST = lax.Precision.HIGHEST
 VMEM = pl.BlockSpec(memory_space=pltpu.VMEM)
+HBM = pl.BlockSpec(memory_space=pltpu.HBM)
 SMEM = pl.BlockSpec(memory_space=pltpu.SMEM)
 PARAMS = pltpu.CompilerParams(vmem_limit_bytes=16 << 20)
 
@@ -36,12 +37,18 @@
     return dot(ah, bh, dims, None) + (dot(al, bh, dims, None) + dot(ah, bl, dims, None))
 
 
-def pack_kernel(where_ref, returns_ref, starts_ref, out_ref):
+def pack_kernel(where_ref, returns_hbm, starts_hbm, out_ref, returns_ref, starts_ref, arrived):
     windows, days, width = returns_ref.shape
     parts = width // LANES
+    copies = [pltpu.make_async_copy(starts_hbm, starts_ref, arrived.at[windows])]
+    copies += [pltpu.make_async_copy(returns_hbm.at[w], returns_ref.at[w], arrived.at[w]) for w in range(windows)]
+    for copy in copies:
+        copy.start()
     day = lax.broadcasted_iota(jnp.int32, (days, width), 0) + where_ref[0] * days
     row = lax.broadcasted_iota(jnp.int32, (QUAD, width), 0)
+    copies[0].wait()
     for w in range(windows):
+        copies[w + 1].wait()
         live = day >= starts_ref[w : w + 1, :]
         kept = jnp.where(live, returns_ref[w], 0.0)
         number = jnp.sum(live.astype(F32), axis=0, keepdims=True)
@@ -214,8 +221,14 @@
     packed = pl.pallas_call(
         pack_kernel,
         out_shape=jax.ShapeDtypeStruct((rows, QUAD, (days // QUAD + 1) * LANES), BF16),
-        in_specs=[SMEM, VMEM, VMEM],
-        out_specs=VMEM,
+        in_specs=[SMEM, HBM, HBM],
+        out_specs=VMEM,
+        scratch_shapes=[
+            pltpu.VMEM(returns.shape, F32),
+            pltpu.VMEM(starts.shape, jnp.int32),
+            pltpu.SemaphoreType.DMA((windows + 1,)),
+        ],
+        compiler_params=PARAMS,
         name="pack",
     )(row[None], returns, starts)
     got = lax.all_to_all(packed, ("window", *part), 0, 0, tiled=True)

time: 170 us -> 171 us (level)
  local copies, waits for them, and re-layouts: 0.07 us -> 1.79 us
    unnamed x4 -> x8, local copies, waits for them, and re-layouts: 0.01 us -> 1.73 us
where the time goes in v7:
time: 171 us; the launch traced here: 170 us
  blocking collectives  80.8 us (47%)
  starting transfers between devices  45.8 us (27%)
  waiting for transfers between devices  33.7 us (20%)
  Pallas kernels  8.23 us (5%)
  local copies, waits for them, and re-layouts  1.79 us (1%)
    all_to_all x1, starting transfers between devices, on_device(): got = lax.all_to_all(packed, ('window', *part), 0, 0, tiled=True)  45.8 us
    all_to_all x1, waiting for transfers between devices, on_device(): got = lax.all_to_all(packed, ('window', *part), 0, 0, tiled=True)  33.7 us
    all_to_all x1, blocking collectives, on_device(): got = lax.all_to_all(sent, ('window', 'far'), 0, 0, tiled=True)  27.7 us
    all_to_all x1, blocking collectives, on_device(): lax.all_to_all(partial.reshape(pieces, share, LANES), block, 0, 0, tiled=...  12.8 us
    all_to_all x1, blocking collectives, on_device(): lax.all_to_all(jnp.broadcast_to(own[None], (pieces, share, LANES)), block...  10.2 us
    all_to_all x1, blocking collectives, on_device(): lax.all_to_all(jnp.broadcast_to(got[None], (NEAR, *got.shape)), quad, 0,...  10.2 us
    all_gather x1, blocking collectives, on_device(): own = lax.all_gather(own, 'far').sum(axis=0)  9.3 us
    all_gather x1, blocking collectives, on_device(): own = lax.all_gather(own, 'mid').sum(axis=0)  6.04 us
  transfers between devices with their start and end apart: 1, of which 1 were waited for; matrix products, arithmetic and copies ran while one was open for 0% of the time, Pallas kernels for 0%

profile of v7, /device:TPU:40, one launch (start us, length us, event | category | flops | bytes accessed | tf_op | source)
XLA Modules:
  0.0 170.4 jit_solution(8405511014560777413)
XLA Ops:
  0.0 0.0 copy-start
  0.0 0.0 copy-start.1
  0.0 1.0 copy-done.1
  1.0 0.0 copy-start.2
  1.0 0.7 copy-done.2
  1.7 1.3 pack.1
  3.0 0.0 copy-start.3
  3.0 45.8 %all-to-all-start = ((bf16[32,4,640]{2,1,0:T(4,128)(2,1)}), bf16[32,4,640]{2,1,0:T(4,128)(2,1)S(1)}, u32[]{:S(2)}, u32[]{:S(2)}) async-start(bf16[32,4,640]{2,1,0:T(4,128)(2,1)} %pack.1), calls=%async_computation | async-start | bytes 327680 | tf_op jit(solution)/shard_map/all_to_all | solution.py:234
  48.8 33.7 %all-to-all-done.got_ref = bf16[32,4,640]{2,1,0:T(4,128)(2,1)S(1)} async-done(((bf16[32,4,640]{2,1,0:T(4,128)(2,1)}), bf16[32,4,640]{2,1,0:T(4,128)(2,1)S(1)}, u32[]{:S(2)}, u32[]{:S(2)}) %all-to-all-start) | async-done | bytes 163872 | tf_op jit(solution)/shard_map/all_to_all | solution.py:234
  82.5 0.0 copy-done
  82.5 0.0 copy-done.3
  82.5 0.3 scale.1.scaled_ref
  82.8 2.3 %all-gather = f32[1088,128]{1,0:T(8,128)S(1)} all-gather(f32[544,128]{1,0:T(8,128)S(1)} %scale.1.scaled_ref), channel_id=2, replica_groups=mesh['groups'=2,'window'=4,'far'=2,'mid'=2,'near'=2,'cols'=4,'sub'=2] {'..., dimensions={0}, use_global_device_ids=true | all-gather | bytes 835584 | tf_op jit(solution)/shard_map/all_gather | solution.py:248
  85.1 0.9 gram.1
  86.0 12.8 %all_to_all.25 = f32[8,80,128]{2,1,0:T(8,128)S(1)} all-to-all(f32[8,80,128]{2,1,0:T(8,128)S(1)} %bitcast.8), channel_id=1, replica_groups=mesh['groups'=2,'window'=4,'far'=2,'mid'=2,'near'=2,'cols'=4,'sub'=2] {'..., dimensions={0} | all-to-all | bytes 655360 | tf_op jit(solution)/shard_map/all_to_all | solution.py:261
  98.8 6.0 %all-gather.1 = f32[160,128]{1,0:T(8,128)S(1)} all-gather(f32[80,128]{1,0:T(8,128)S(1)} %reduce_sum.27), channel_id=3, replica_groups=mesh['groups'=2,'window'=4,'far'=2,'mid'=2,'near'=2,'cols'=4,'sub'=2] {'..., dimensions={0}, use_global_device_ids=true | all-gather | bytes 122880 | tf_op jit(solution)/shard_map/all_gather | solution.py:262
  104.9 9.3 %all-gather.2 = f32[160,128]{1,0:T(8,128)S(1)} all-gather(f32[80,128]{1,0:T(8,128)S(1)} %reduce_sum.28), channel_id=4, replica_groups=mesh['groups'=2,'window'=4,'far'=2,'mid'=2,'near'=2,'cols'=4,'sub'=2] {'..., dimensions={0}, use_global_device_ids=true | all-gather | bytes 122880 | tf_op jit(solution)/shard_map/all_gather | solution.py:263
  114.2 10.2 %all_to_all.26 = f32[8,80,128]{2,1,0:T(8,128)S(1)} all-to-all(f32[8,80,128]{2,1,0:T(8,128)S(1)} %broadcast_in_dim.10), channel_id=1, replica_groups=mesh['groups'=2,'window'=4,'far'=2,'mid'=2,'near'=2,'cols'=4,'sub'=2] {'..., dimensions={0} | all-to-all | bytes 655360 | tf_op jit(solution)/shard_map/all_to_all | solution.py:264
  124.5 2.3 %all_gather.27.got_ref = f32[1280,128]{1,0:T(8,128)S(1)} all-gather(f32[640,128]{1,0:T(8,128)S(1)} %bitcast.9), channel_id=1, replica_groups=mesh['groups'=2,'window'=4,'far'=2,'mid'=2,'near'=2,'cols'=4,'sub'=2] {'..., dimensions={0}, use_global_device_ids=true | all-gather | bytes 983040 | tf_op jit(solution)/shard_map/all_gather | solution.py:265
  126.8 4.9 %iterate.1 = bf16[8,32,128]{2,1,0:T(8,128)(2,1)S(1)} custom-call(f32[1280,128]{1,0:T(8,128)S(1)} %all_gather.27.got_ref, f32[544,128]{1,0:T(8,128)S(1)} %scale.1.scaled_ref), custom_call_target="tpu_custom_call" | custom-call | tf_op jit(solution)/shard_map/iterate/pallas_call | solution.py:268
  131.6 27.7 %all_to_all.27 = bf16[8,32,128]{2,1,0:T(8,128)(2,1)S(1)} all-to-all(bf16[8,32,128]{2,1,0:T(8,128)(2,1)S(1)} %iterate.1), channel_id=1, replica_groups=mesh['groups'=2,'window'=4,'far'=2,'mid'=2,'near'=2,'cols'=4,'sub'=2] {'..., dimensions={0} | all-to-all | bytes 131072 | tf_op jit(solution)/shard_map/all_to_all | solution.py:277
  159.4 10.2 %all_to_all.28.got_ref = bf16[4,8,32,128]{3,2,1,0:T(8,128)(2,1)S(1)} all-to-all(bf16[4,8,32,128]{3,2,1,0:T(8,128)(2,1)S(1)} %broadcast_in_dim.22), channel_id=1, replica_groups=mesh['groups'=2,'window'=4,'far'=2,'mid'=2,'near'=2,'cols'=4,'sub'=2] {'..., dimensions={0} | all-to-all | bytes 524288 | tf_op jit(solution)/shard_map/all_to_all | solution.py:278
  169.6 0.8 unpack.1
  (5 shorter events, 0.1 us)
Async XLA Ops:
  0.0 82.5 %copy-start = (f32[4,32,1024]{2,1,0:T(8,128)S(1)}, f32[4,32,1024]{2,1,0:T(8,128)}, u32[]{:S(2)}) copy-start(f32[4,32,1024]{2,1,0:T(8,128)} %block_ref.1) | copy-start | bytes 1572868
  0.0 1.0 copy-start.1
  1.0 0.7 copy-start.2
  3.0 79.5 %copy-start.3 = (s32[4,1024]{1,0:T(4,128)S(1)}, s32[4,1024]{1,0:T(4,128)}, u32[]{:S(2)}) copy-start(s32[4,1024]{1,0:T(4,128)} %starts_ref.1) | copy-start | bytes 49156
  3.0 79.5 %all-to-all-start = ((bf16[32,4,640]{2,1,0:T(4,128)(2,1)}), bf16[32,4,640]{2,1,0:T(4,128)(2,1)S(1)}, u32[]{:S(2)}, u32[]{:S(2)}) async-start(bf16[32,4,640]{2,1,0:T(4,128)(2,1)} %pack.1), calls=%async_computation | async-start | bytes 327680 | tf_op jit(solution)/shard_map/all_to_all | solution.py:234

commit v8 on v7

--- a/solution.py
+++ b/solution.py
@@ -199,11 +199,11 @@
 
 def unpack_kernel(got_ref, out_ref):
     windows, _, width = out_ref.shape
-    near, blocks = got_ref.shape[:2]
+    near, mid, blocks = got_ref.shape[:3]
     for w in range(windows):
         for j in range(width // LANES):
-            block = w * (blocks // windows) + j // near
-            out_ref[w, :, j * LANES : (j + 1) * LANES] = got_ref[j % near, block].astype(F32)
+            block = w * (blocks // windows) + j // (mid * near)
+            out_ref[w, :, j * LANES : (j + 1) * LANES] = got_ref[j % near, j // near % mid, block].astype(F32)
 
 
 def on_device(returns, starts, start_block):
@@ -215,7 +215,7 @@
     sides = cols * sub
     total = days * rows
     assets = width * sides
-    part, quad, block = ("far", "mid", "near"), ("mid", "near"), ("near", "cols")
+    part, block = ("far", "mid", "near"), ("near", "cols")
     row = lax.axis_index("window") * parts + lax.axis_index(part)
 
     packed = pl.pallas_call(
@@ -228,7 +228,6 @@
             pltpu.VMEM(starts.shape, jnp.int32),
             pltpu.SemaphoreType.DMA((windows + 1,)),
         ],
-        compiler_params=PARAMS,
         name="pack",
     )(row[None], returns, starts)
     got = lax.all_to_all(packed, ("window", *part), 0, 0, tiled=True)
@@ -275,7 +274,7 @@
         name="iterate",
     )(whole, scaled)
     got = lax.all_to_all(sent, ("window", "far"), 0, 0, tiled=True)
-    got = lax.all_to_all(jnp.broadcast_to(got[None], (NEAR, *got.shape)), quad, 0, 0, tiled=True)
+    got = lax.all_gather(lax.all_gather(got, "mid"), "near")
     return pl.pallas_call(
         unpack_kernel,
         out_shape=jax.ShapeDtypeStruct((windows, factors, width), F32),

time: 171 us -> 171 us (level)
  local copies, waits for them, and re-layouts: 1.79 us -> 0.03 us
    all_gather x0 -> x2, blocking collectives: none -> 11.5 us  [on_device(): got = lax.all_gather(lax.all_gather(got, 'mid'), 'near')]
    all_to_all x1 -> x0, blocking collectives: 10.2 us -> none  [on_device(): lax.all_to_all(jnp.broadcast_to(got[None], (NEAR, *got.shape)), quad, 0,...]
    unnamed x8 -> x4, local copies, waits for them, and re-layouts: 1.73 us -> 0.01 us
where the time goes in v8:
time: 171 us
  blocking collectives  82.1 us (48%)
  starting transfers between devices  45.8 us (27%)
  waiting for transfers between devices  33.7 us (20%)
  Pallas kernels  8.81 us (5%)
    all_to_all x1, starting transfers between devices, on_device(): got = lax.all_to_all(packed, ('window', *part), 0, 0, tiled=True)  45.8 us
    all_to_all x1, waiting for transfers between devices, on_device(): got = lax.all_to_all(packed, ('window', *part), 0, 0, tiled=True)  33.7 us
    all_to_all x1, blocking collectives, on_device(): got = lax.all_to_all(sent, ('window', 'far'), 0, 0, tiled=True)  27.7 us
    all_to_all x1, blocking collectives, on_device(): lax.all_to_all(partial.reshape(pieces, share, LANES), block, 0, 0, tiled=...  12.8 us
    all_gather x2, blocking collectives, on_device(): got = lax.all_gather(lax.all_gather(got, 'mid'), 'near')  11.5 us
    all_to_all x1, blocking collectives, on_device(): lax.all_to_all(jnp.broadcast_to(own[None], (pieces, share, LANES)), block...  10.2 us
    all_gather x1, blocking collectives, on_device(): own = lax.all_gather(own, 'far').sum(axis=0)  9.31 us
    all_gather x1, blocking collectives, on_device(): own = lax.all_gather(own, 'mid').sum(axis=0)  6.04 us
  transfers between devices with their start and end apart: 1, of which 1 were waited for; matrix products, arithmetic and copies ran while one was open for 0% of the time, Pallas kernels for 0%

profile of v8, /device:TPU:40, one launch (start us, length us, event | category | flops | bytes accessed | tf_op | source)
XLA Modules:
  0.0 170.5 jit_solution(386894430943369336)
XLA Ops:
  0.0 0.0 copy-start
  0.0 1.9 %pack.1 = bf16[32,4,640]{2,1,0:T(4,128)(2,1)} custom-call(s32[1]{0:T(128)} %bitcast.1.where_ref, f32[4,16,1024]{2,1,0:T(8,128)} %returns_hbm.1, s32[4,1024]{1,0:T(4,128)} %starts_ref.1), custom_call_target="tpu_custom_call" | custom-call | tf_op jit(solution)/shard_map/pack/pallas_call | solution.py:221
  1.9 0.0 copy-start.1
  1.9 45.8 %all-to-all-start = ((bf16[32,4,640]{2,1,0:T(4,128)(2,1)}), bf16[32,4,640]{2,1,0:T(4,128)(2,1)S(1)}, u32[]{:S(2)}, u32[]{:S(2)}) async-start(bf16[32,4,640]{2,1,0:T(4,128)(2,1)} %pack.1), calls=%async_computation | async-start | bytes 327680 | tf_op jit(solution)/shard_map/all_to_all | solution.py:233
  47.7 33.7 %all-to-all-done.got_ref = bf16[32,4,640]{2,1,0:T(4,128)(2,1)S(1)} async-done(((bf16[32,4,640]{2,1,0:T(4,128)(2,1)}), bf16[32,4,640]{2,1,0:T(4,128)(2,1)S(1)}, u32[]{:S(2)}, u32[]{:S(2)}) %all-to-all-start) | async-done | bytes 163872 | tf_op jit(solution)/shard_map/all_to_all | solution.py:233
  81.4 0.0 copy-done
  81.4 0.0 copy-done.1
  81.4 0.3 scale.1.scaled_ref
  81.7 2.3 %all-gather = f32[1088,128]{1,0:T(8,128)S(1)} all-gather(f32[544,128]{1,0:T(8,128)S(1)} %scale.1.scaled_ref), channel_id=2, replica_groups=mesh['groups'=2,'window'=4,'far'=2,'mid'=2,'near'=2,'cols'=4,'sub'=2] {'..., dimensions={0}, use_global_device_ids=true | all-gather | bytes 835584 | tf_op jit(solution)/shard_map/all_gather | solution.py:247
  83.9 1.0 gram.1
  84.9 12.8 %all_to_all.20 = f32[8,80,128]{2,1,0:T(8,128)S(1)} all-to-all(f32[8,80,128]{2,1,0:T(8,128)S(1)} %bitcast.10), channel_id=1, replica_groups=mesh['groups'=2,'window'=4,'far'=2,'mid'=2,'near'=2,'cols'=4,'sub'=2] {'..., dimensions={0} | all-to-all | bytes 655360 | tf_op jit(solution)/shard_map/all_to_all | solution.py:260
  97.7 6.0 %all-gather.1 = f32[160,128]{1,0:T(8,128)S(1)} all-gather(f32[80,128]{1,0:T(8,128)S(1)} %reduce_sum.27), channel_id=3, replica_groups=mesh['groups'=2,'window'=4,'far'=2,'mid'=2,'near'=2,'cols'=4,'sub'=2] {'..., dimensions={0}, use_global_device_ids=true | all-gather | bytes 122880 | tf_op jit(solution)/shard_map/all_gather | solution.py:261
  103.7 9.3 %all-gather.2 = f32[160,128]{1,0:T(8,128)S(1)} all-gather(f32[80,128]{1,0:T(8,128)S(1)} %reduce_sum.28), channel_id=4, replica_groups=mesh['groups'=2,'window'=4,'far'=2,'mid'=2,'near'=2,'cols'=4,'sub'=2] {'..., dimensions={0}, use_global_device_ids=true | all-gather | bytes 122880 | tf_op jit(solution)/shard_map/all_gather | solution.py:262
  113.1 10.2 %all_to_all.21 = f32[8,80,128]{2,1,0:T(8,128)S(1)} all-to-all(f32[8,80,128]{2,1,0:T(8,128)S(1)} %broadcast_in_dim.15), channel_id=1, replica_groups=mesh['groups'=2,'window'=4,'far'=2,'mid'=2,'near'=2,'cols'=4,'sub'=2] {'..., dimensions={0} | all-to-all | bytes 655360 | tf_op jit(solution)/shard_map/all_to_all | solution.py:263
  123.3 2.3 %all_gather.39.got_ref = f32[1280,128]{1,0:T(8,128)S(1)} all-gather(f32[640,128]{1,0:T(8,128)S(1)} %bitcast.12), channel_id=1, replica_groups=mesh['groups'=2,'window'=4,'far'=2,'mid'=2,'near'=2,'cols'=4,'sub'=2] {'..., dimensions={0}, use_global_device_ids=true | all-gather | bytes 983040 | tf_op jit(solution)/shard_map/all_gather | solution.py:264
  125.6 4.9 %iterate.1 = bf16[8,32,128]{2,1,0:T(8,128)(2,1)S(1)} custom-call(f32[1280,128]{1,0:T(8,128)S(1)} %all_gather.39.got_ref, f32[544,128]{1,0:T(8,128)S(1)} %scale.1.scaled_ref), custom_call_target="tpu_custom_call" | custom-call | tf_op jit(solution)/shard_map/iterate/pallas_call | solution.py:267
  130.5 27.7 %all_to_all.22 = bf16[8,32,128]{2,1,0:T(8,128)(2,1)S(1)} all-to-all(bf16[8,32,128]{2,1,0:T(8,128)(2,1)S(1)} %iterate.1), channel_id=1, replica_groups=mesh['groups'=2,'window'=4,'far'=2,'mid'=2,'near'=2,'cols'=4,'sub'=2] {'..., dimensions={0} | all-to-all | bytes 131072 | tf_op jit(solution)/shard_map/all_to_all | solution.py:276
  158.2 5.8 %all-gather.3 = bf16[16,32,128]{2,1,0:T(8,128)(2,1)S(1)} all-gather(bf16[8,32,128]{2,1,0:T(8,128)(2,1)S(1)} %all_to_all.22), channel_id=5, replica_groups=mesh['groups'=2,'window'=4,'far'=2,'mid'=2,'near'=2,'cols'=4,'sub'=2] {'..., dimensions={0}, use_global_device_ids=true | all-gather | bytes 196608 | tf_op jit(solution)/shard_map/all_gather | solution.py:277
  164.1 5.6 %all-gather.4 = bf16[4,8,32,128]{3,2,1,0:T(8,128)(2,1)S(1)} all-gather(bf16[2,8,32,128]{3,2,1,0:T(8,128)(2,1)S(1)} %bitcast.13), channel_id=6, replica_groups=mesh['groups'=2,'window'=4,'far'=2,'mid'=2,'near'=2,'cols'=4,'sub'=2] {'..., dimensions={0}, use_global_device_ids=true | all-gather | bytes 393216 | tf_op jit(solution)/shard_map/all_gather | solution.py:277
  169.7 0.8 unpack.1
  (4 shorter events, 0.1 us)
Async XLA Ops:
  0.0 81.4 %copy-start = (f32[4,32,1024]{2,1,0:T(8,128)S(1)}, f32[4,32,1024]{2,1,0:T(8,128)}, u32[]{:S(2)}) copy-start(f32[4,32,1024]{2,1,0:T(8,128)} %block_ref.1) | copy-start | bytes 1572868
  1.9 79.5 %copy-start.1 = (s32[4,1024]{1,0:T(4,128)S(1)}, s32[4,1024]{1,0:T(4,128)}, u32[]{:S(2)}) copy-start(s32[4,1024]{1,0:T(4,128)} %starts_ref.1) | copy-start | bytes 49156
  1.9 79.5 %all-to-all-start = ((bf16[32,4,640]{2,1,0:T(4,128)(2,1)}), bf16[32,4,640]{2,1,0:T(4,128)(2,1)S(1)}, u32[]{:S(2)}, u32[]{:S(2)}) async-start(bf16[32,4,640]{2,1,0:T(4,128)(2,1)} %pack.1), calls=%async_computation | async-start | bytes 327680 | tf_op jit(solution)/shard_map/all_to_all | solution.py:233

commit v9 on v6

--- a/solution.py
+++ b/solution.py
@@ -10,6 +10,7 @@
 
 ITERS = 3
 LANES = 128
+ROWS = ("window", "far", "mid", "near")
 HALF = LANES // 2
 NEAR = 4
 EIGHT = 8
@@ -18,7 +19,6 @@
 BF16 = jnp.bfloat16
 HIGHEST = lax.Precision.HIGHEST
 VMEM = pl.BlockSpec(memory_space=pltpu.VMEM)
-SMEM = pl.BlockSpec(memory_space=pltpu.SMEM)
 PARAMS = pltpu.CompilerParams(vmem_limit_bytes=16 << 20)
 
 
@@ -36,10 +36,10 @@
     return dot(ah, bh, dims, None) + (dot(al, bh, dims, None) + dot(ah, bl, dims, None))
 
 
-def pack_kernel(where_ref, returns_ref, starts_ref, out_ref):
+def pack_kernel(returns_ref, starts_ref, out_ref):
     windows, days, width = returns_ref.shape
     parts = width // LANES
-    day = lax.broadcasted_iota(jnp.int32, (days, width), 0) + where_ref[0] * days
+    day = lax.broadcasted_iota(jnp.int32, (days, width), 0) + lax.axis_index(ROWS) * days
     row = lax.broadcasted_iota(jnp.int32, (QUAD, width), 0)
     for w in range(windows):
         live = day >= starts_ref[w : w + 1, :]
@@ -59,13 +59,13 @@
                 out_ref[w * parts + j, :, i * LANES : (i + 1) * LANES] = block[:, j * LANES : (j + 1) * LANES]
 
 
-def scale_kernel(where_ref, got_ref, starts_ref, block_ref, out_ref):
+def scale_kernel(got_ref, starts_ref, block_ref, out_ref):
     sources = got_ref.shape[0]
     days = (got_ref.shape[2] // LANES - 1) * QUAD
     total = sources * days
     parts = sources // starts_ref.shape[0]
-    w = where_ref[0] // parts
-    own = pl.ds(pl.multiple_of(where_ref[0] % parts * LANES, LANES), LANES)
+    w = lax.axis_index("window")
+    own = pl.ds(pl.multiple_of(lax.axis_index(ROWS) % parts * LANES, LANES), LANES)
     starts = starts_ref[:, own]
     starts = jnp.sum(jnp.where(lax.broadcasted_iota(jnp.int32, starts.shape, 0) == w, starts, 0), axis=0, keepdims=True)
     got = got_ref[...].astype(F32)
@@ -85,7 +85,7 @@
     out_ref[total:, :] = block_ref[w, :, own].astype(BF16).astype(F32)
 
 
-def gram_kernel(where_ref, both_ref, out_ref, all_ref):
+def gram_kernel(both_ref, out_ref, all_ref):
     cores, rows, _ = both_ref.shape
     total = rows // LANES * LANES
     both = jnp.concatenate([both_ref[c] for c in range(cores)], axis=1)
@@ -118,7 +118,7 @@
     if at < all_ref.shape[0]:
         all_ref[at:, :] = jnp.zeros((all_ref.shape[0] - at, LANES), F32)
     share = out_ref.shape[0]
-    out_ref[...] = all_ref[pl.ds(pl.multiple_of(where_ref[0] * share, EIGHT), share), :]
+    out_ref[...] = all_ref[pl.ds(pl.multiple_of(lax.axis_index("sub") * share, EIGHT), share), :]
 
 
 def inverse_lower(gram):
@@ -208,17 +208,16 @@
     sides = cols * sub
     total = days * rows
     assets = width * sides
-    part, quad, block = ("far", "mid", "near"), ("mid", "near"), ("near", "cols")
-    row = lax.axis_index("window") * parts + lax.axis_index(part)
+    quad, block = ("mid", "near"), ("near", "cols")
 
     packed = pl.pallas_call(
         pack_kernel,
         out_shape=jax.ShapeDtypeStruct((rows, QUAD, (days // QUAD + 1) * LANES), BF16),
-        in_specs=[SMEM, VMEM, VMEM],
+        in_specs=[VMEM, VMEM],
         out_specs=VMEM,
         name="pack",
-    )(row[None], returns, starts)
-    got = lax.all_to_all(packed, ("window", *part), 0, 0, tiled=True)
+    )(returns, starts)
+    got = lax.all_to_all(packed, ROWS, 0, 0, tiled=True)
 
     blocks = total // LANES
     filled = blocks * (blocks - 1) // 2 * LANES + blocks // 2 * 3 * HALF + factors * blocks
@@ -227,21 +226,21 @@
     scaled = pl.pallas_call(
         scale_kernel,
         out_shape=jax.ShapeDtypeStruct((total + factors, LANES), F32),
-        in_specs=[SMEM, VMEM, VMEM, VMEM],
+        in_specs=[VMEM, VMEM, VMEM],
         out_specs=VMEM,
         compiler_params=PARAMS,
         name="scale",
-    )(row[None], got, starts, start_block)
+    )(got, starts, start_block)
     both = lax.all_gather(scaled, "sub")
     partial = pl.pallas_call(
         gram_kernel,
         out_shape=jax.ShapeDtypeStruct((height // sub, LANES), F32),
-        in_specs=[SMEM, VMEM],
+        in_specs=[VMEM],
         out_specs=VMEM,
         scratch_shapes=[pltpu.VMEM((height, LANES), F32)],
         compiler_params=PARAMS,
         name="gram",
-    )(lax.axis_index("sub")[None], both)
+    )(both)
 
     pieces = lax.axis_size(block)
     share = height // sub // pieces

time: 170 us -> 170 us (level)
  blocking collectives: 80.8 us -> 160 us
  starting transfers between devices: 45.9 us -> 0 us
  waiting for transfers between devices: 33.7 us -> 0 us
    all_to_all x0 -> x1, blocking collectives: none -> 79.6 us  [on_device(): got = lax.all_to_all(packed, ROWS, 0, 0, tiled=True)]
    all_to_all x1 -> x0, starting transfers between devices: 45.9 us -> none  [on_device(): got = lax.all_to_all(packed, ('window', *part), 0, 0, tiled=True)]
    all_to_all x1 -> x0, waiting for transfers between devices: 33.7 us -> none  [on_device(): got = lax.all_to_all(packed, ('window', *part), 0, 0, tiled=True)]
  transfers between devices with their start and end apart: 1 -> 0, of which waited for: 1 -> 0; matrix products, arithmetic and copies ran while one was open for 0% -> 0% of each run, Pallas kernels for 0% -> 0%
where the time goes in v9:
time: 170 us; the launch traced here: 169 us
  blocking collectives  160 us (94%)
  Pallas kernels  8.83 us (5%)
    all_to_all x1, blocking collectives, on_device(): got = lax.all_to_all(packed, ROWS, 0, 0, tiled=True)  79.6 us
    all_to_all x1, blocking collectives, on_device(): got = lax.all_to_all(sent, ('window', 'far'), 0, 0, tiled=True)  27.7 us
    all_to_all x1, blocking collectives, on_device(): lax.all_to_all(partial.reshape(pieces, share, LANES), block, 0, 0, tiled=...  12.8 us
    all_to_all x1, blocking collectives, on_device(): lax.all_to_all(jnp.broadcast_to(own[None], (pieces, share, LANES)), block...  10.2 us
    all_to_all x1, blocking collectives, on_device(): lax.all_to_all(jnp.broadcast_to(got[None], (NEAR, *got.shape)), quad, 0,...  10.2 us
    all_gather x1, blocking collectives, on_device(): own = lax.all_gather(own, 'far').sum(axis=0)  9.31 us
    all_gather x1, blocking collectives, on_device(): own = lax.all_gather(own, 'mid').sum(axis=0)  6.04 us
    pallas_call x1, Pallas kernels, on_device(): pl.pallas_call(functools.partial(iterate_kernel, assets), out_shape=jax.S...  4.89 us

profile of v9, /device:TPU:40, one launch (start us, length us, event | category | flops | bytes accessed | tf_op | source)
XLA Modules:
  0.0 169.4 jit_solution(17803100065774034219)
XLA Ops:
  0.0 0.0 copy-start
  0.0 1.9 %pack.1 = bf16[32,4,640]{2,1,0:T(4,128)(2,1)} custom-call(f32[4,16,1024]{2,1,0:T(8,128)} %returns_ref.1, s32[4,1024]{1,0:T(4,128)} %starts_ref.3), custom_call_target="tpu_custom_call" | custom-call | tf_op jit(solution)/shard_map/pack/pallas_call | solution.py:213
  1.9 0.0 copy-start.1
  1.9 79.6 %all_to_all.25.got_ref = bf16[32,4,640]{2,1,0:T(4,128)(2,1)S(1)} all-to-all(bf16[32,4,640]{2,1,0:T(4,128)(2,1)} %pack.1), channel_id=1, replica_groups=mesh['groups'=2,'window'=4,'far'=2,'mid'=2,'near'=2,'cols'=4,'sub'=2] {'..., dimensions={0} | all-to-all | bytes 327680 | tf_op jit(solution)/shard_map/all_to_all | solution.py:220
  81.5 0.0 copy-done
  81.5 0.0 copy-done.1
  81.5 0.3 scale.1.scaled_ref
  81.8 2.3 %all-gather = f32[1088,128]{1,0:T(8,128)S(1)} all-gather(f32[544,128]{1,0:T(8,128)S(1)} %scale.1.scaled_ref), channel_id=2, replica_groups=mesh['groups'=2,'window'=4,'far'=2,'mid'=2,'near'=2,'cols'=4,'sub'=2] {'..., dimensions={0}, use_global_device_ids=true | all-gather | bytes 835584 | tf_op jit(solution)/shard_map/all_gather | solution.py:234
  84.1 0.9 gram.1
  85.0 12.8 %all_to_all.26 = f32[8,80,128]{2,1,0:T(8,128)S(1)} all-to-all(f32[8,80,128]{2,1,0:T(8,128)S(1)} %bitcast.6), channel_id=1, replica_groups=mesh['groups'=2,'window'=4,'far'=2,'mid'=2,'near'=2,'cols'=4,'sub'=2] {'..., dimensions={0} | all-to-all | bytes 655360 | tf_op jit(solution)/shard_map/all_to_all | solution.py:247
  97.8 6.0 %all-gather.1 = f32[160,128]{1,0:T(8,128)S(1)} all-gather(f32[80,128]{1,0:T(8,128)S(1)} %reduce_sum.27), channel_id=3, replica_groups=mesh['groups'=2,'window'=4,'far'=2,'mid'=2,'near'=2,'cols'=4,'sub'=2] {'..., dimensions={0}, use_global_device_ids=true | all-gather | bytes 122880 | tf_op jit(solution)/shard_map/all_gather | solution.py:248
  103.9 9.3 %all-gather.2 = f32[160,128]{1,0:T(8,128)S(1)} all-gather(f32[80,128]{1,0:T(8,128)S(1)} %reduce_sum.28), channel_id=4, replica_groups=mesh['groups'=2,'window'=4,'far'=2,'mid'=2,'near'=2,'cols'=4,'sub'=2] {'..., dimensions={0}, use_global_device_ids=true | all-gather | bytes 122880 | tf_op jit(solution)/shard_map/all_gather | solution.py:249
  113.2 10.2 %all_to_all.27 = f32[8,80,128]{2,1,0:T(8,128)S(1)} all-to-all(f32[8,80,128]{2,1,0:T(8,128)S(1)} %broadcast_in_dim.4), channel_id=1, replica_groups=mesh['groups'=2,'window'=4,'far'=2,'mid'=2,'near'=2,'cols'=4,'sub'=2] {'..., dimensions={0} | all-to-all | bytes 655360 | tf_op jit(solution)/shard_map/all_to_all | solution.py:250
  123.4 2.3 %all_gather.27.got_ref = f32[1280,128]{1,0:T(8,128)S(1)} all-gather(f32[640,128]{1,0:T(8,128)S(1)} %bitcast.7), channel_id=1, replica_groups=mesh['groups'=2,'window'=4,'far'=2,'mid'=2,'near'=2,'cols'=4,'sub'=2] {'..., dimensions={0}, use_global_device_ids=true | all-gather | bytes 983040 | tf_op jit(solution)/shard_map/all_gather | solution.py:251
  125.7 4.9 %iterate.1 = bf16[8,32,128]{2,1,0:T(8,128)(2,1)S(1)} custom-call(f32[1280,128]{1,0:T(8,128)S(1)} %all_gather.27.got_ref, f32[544,128]{1,0:T(8,128)S(1)} %scale.1.scaled_ref), custom_call_target="tpu_custom_call" | custom-call | tf_op jit(solution)/shard_map/iterate/pallas_call | solution.py:254
  130.6 27.7 %all_to_all.28 = bf16[8,32,128]{2,1,0:T(8,128)(2,1)S(1)} all-to-all(bf16[8,32,128]{2,1,0:T(8,128)(2,1)S(1)} %iterate.1), channel_id=1, replica_groups=mesh['groups'=2,'window'=4,'far'=2,'mid'=2,'near'=2,'cols'=4,'sub'=2] {'..., dimensions={0} | all-to-all | bytes 131072 | tf_op jit(solution)/shard_map/all_to_all | solution.py:263
  158.4 10.2 %all_to_all.29.got_ref = bf16[4,8,32,128]{3,2,1,0:T(8,128)(2,1)S(1)} all-to-all(bf16[4,8,32,128]{3,2,1,0:T(8,128)(2,1)S(1)} %broadcast_in_dim.5), channel_id=1, replica_groups=mesh['groups'=2,'window'=4,'far'=2,'mid'=2,'near'=2,'cols'=4,'sub'=2] {'..., dimensions={0} | all-to-all | bytes 524288 | tf_op jit(solution)/shard_map/all_to_all | solution.py:264
  168.5 0.8 unpack.1
  (5 shorter events, 0.1 us)
Async XLA Ops:
  0.0 81.5 %copy-start = (f32[4,32,1024]{2,1,0:T(8,128)S(1)}, f32[4,32,1024]{2,1,0:T(8,128)}, u32[]{:S(2)}) copy-start(f32[4,32,1024]{2,1,0:T(8,128)} %block_ref.1) | copy-start | bytes 1572868
  1.9 79.6 %copy-start.1 = (s32[4,1024]{1,0:T(4,128)S(1)}, s32[4,1024]{1,0:T(4,128)}, u32[]{:S(2)}) copy-start(s32[4,1024]{1,0:T(4,128)} %starts_ref.3) | copy-start | bytes 49156

commit v10 on v9

--- a/solution.py
+++ b/solution.py
@@ -245,8 +245,8 @@
     pieces = lax.axis_size(block)
     share = height // sub // pieces
     own = lax.all_to_all(partial.reshape(pieces, share, LANES), block, 0, 0, tiled=True).sum(axis=0)
-    own = lax.all_gather(own, "mid").sum(axis=0)
-    own = lax.all_gather(own, "far").sum(axis=0)
+    even = ("far", "mid")
+    own = lax.all_to_all(jnp.broadcast_to(own[None], (lax.axis_size(even), share, LANES)), even, 0, 0, tiled=True).sum(axis=0)
     own = lax.all_to_all(jnp.broadcast_to(own[None], (pieces, share, LANES)), block, 0, 0, tiled=True)
     whole = lax.all_gather(own.reshape(height // sub, LANES), "sub", tiled=True)
 

time: 170 us -> 174 us (1.024)
  blocking collectives: 160 us -> 164 us
    all_gather x2 -> x0, blocking collectives: 15.4 us -> none  [the longest x1 9.31 us: on_device(): own = lax.all_gather(own, 'far').sum(axis=0)]
    all_to_all x0 -> x1, blocking collectives: none -> 14.9 us  [on_device(): lax.all_to_all(jnp.broadcast_to(own[None], (lax.axis_size(even), share, L...]
    all_to_all x1, blocking collectives: 27.7 us -> 31.9 us  [on_device(): got = lax.all_to_all(sent, ('window', 'far'), 0, 0, tiled=True)]
where the time goes in v10:
time: 174 us; the launch traced here: 173 us
  blocking collectives  164 us (94%)
  Pallas kernels  8.83 us (5%)
    all_to_all x1, blocking collectives, on_device(): got = lax.all_to_all(packed, ROWS, 0, 0, tiled=True)  79.6 us
    all_to_all x1, blocking collectives, on_device(): got = lax.all_to_all(sent, ('window', 'far'), 0, 0, tiled=True)  31.9 us
    all_to_all x1, blocking collectives, on_device(): lax.all_to_all(jnp.broadcast_to(own[None], (lax.axis_size(even), share, L...  14.9 us
    all_to_all x1, blocking collectives, on_device(): lax.all_to_all(partial.reshape(pieces, share, LANES), block, 0, 0, tiled=...  12.8 us
    all_to_all x1, blocking collectives, on_device(): lax.all_to_all(jnp.broadcast_to(got[None], (NEAR, *got.shape)), quad, 0,...  10.5 us
    all_to_all x1, blocking collectives, on_device(): lax.all_to_all(jnp.broadcast_to(own[None], (pieces, share, LANES)), block...  10.2 us
    pallas_call x1, Pallas kernels, on_device(): pl.pallas_call(functools.partial(iterate_kernel, assets), out_shape=jax.S...  4.88 us

profile of v10, /device:TPU:40, one launch (start us, length us, event | category | flops | bytes accessed | tf_op | source)
XLA Modules:
  0.0 173.4 jit_solution(9336282825089426052)
XLA Ops:
  0.0 0.0 copy-start
  0.0 1.9 %pack.1 = bf16[32,4,640]{2,1,0:T(4,128)(2,1)} custom-call(f32[4,16,1024]{2,1,0:T(8,128)} %returns_ref.1, s32[4,1024]{1,0:T(4,128)} %starts_ref.3), custom_call_target="tpu_custom_call" | custom-call | tf_op jit(solution)/shard_map/pack/pallas_call | solution.py:213
  1.9 0.0 copy-start.1
  1.9 79.6 %all_to_all.30.got_ref = bf16[32,4,640]{2,1,0:T(4,128)(2,1)S(1)} all-to-all(bf16[32,4,640]{2,1,0:T(4,128)(2,1)} %pack.1), channel_id=1, replica_groups=mesh['groups'=2,'window'=4,'far'=2,'mid'=2,'near'=2,'cols'=4,'sub'=2] {'..., dimensions={0} | all-to-all | bytes 327680 | tf_op jit(solution)/shard_map/all_to_all | solution.py:220
  81.5 0.0 copy-done
  81.5 0.0 copy-done.1
  81.5 0.3 scale.1.scaled_ref
  81.8 2.3 %all-gather = f32[1088,128]{1,0:T(8,128)S(1)} all-gather(f32[544,128]{1,0:T(8,128)S(1)} %scale.1.scaled_ref), channel_id=2, replica_groups=mesh['groups'=2,'window'=4,'far'=2,'mid'=2,'near'=2,'cols'=4,'sub'=2] {'..., dimensions={0}, use_global_device_ids=true | all-gather | bytes 835584 | tf_op jit(solution)/shard_map/all_gather | solution.py:234
  84.1 0.9 gram.1
  85.0 12.8 %all_to_all.31 = f32[8,80,128]{2,1,0:T(8,128)S(1)} all-to-all(f32[8,80,128]{2,1,0:T(8,128)S(1)} %bitcast.4), channel_id=1, replica_groups=mesh['groups'=2,'window'=4,'far'=2,'mid'=2,'near'=2,'cols'=4,'sub'=2] {'..., dimensions={0} | all-to-all | bytes 655360 | tf_op jit(solution)/shard_map/all_to_all | solution.py:247
  97.8 14.9 %all_to_all.32 = f32[4,80,128]{2,1,0:T(8,128)S(1)} all-to-all(f32[4,80,128]{2,1,0:T(8,128)S(1)} %broadcast_in_dim.6), channel_id=1, replica_groups=mesh['groups'=2,'window'=4,'far'=2,'mid'=2,'near'=2,'cols'=4,'sub'=2] {'..., dimensions={0} | all-to-all | bytes 327680 | tf_op jit(solution)/shard_map/all_to_all | solution.py:249
  112.8 10.2 %all_to_all.33 = f32[8,80,128]{2,1,0:T(8,128)S(1)} all-to-all(f32[8,80,128]{2,1,0:T(8,128)S(1)} %broadcast_in_dim.7), channel_id=1, replica_groups=mesh['groups'=2,'window'=4,'far'=2,'mid'=2,'near'=2,'cols'=4,'sub'=2] {'..., dimensions={0} | all-to-all | bytes 655360 | tf_op jit(solution)/shard_map/all_to_all | solution.py:250
  123.0 2.3 %all_gather.11.got_ref = f32[1280,128]{1,0:T(8,128)S(1)} all-gather(f32[640,128]{1,0:T(8,128)S(1)} %bitcast.5), channel_id=1, replica_groups=mesh['groups'=2,'window'=4,'far'=2,'mid'=2,'near'=2,'cols'=4,'sub'=2] {'..., dimensions={0}, use_global_device_ids=true | all-gather | bytes 983040 | tf_op jit(solution)/shard_map/all_gather | solution.py:251
  125.3 4.9 %iterate.1 = bf16[8,32,128]{2,1,0:T(8,128)(2,1)S(1)} custom-call(f32[1280,128]{1,0:T(8,128)S(1)} %all_gather.11.got_ref, f32[544,128]{1,0:T(8,128)S(1)} %scale.1.scaled_ref), custom_call_target="tpu_custom_call" | custom-call | tf_op jit(solution)/shard_map/iterate/pallas_call | solution.py:254
  130.2 31.9 %all_to_all.34 = bf16[8,32,128]{2,1,0:T(8,128)(2,1)S(1)} all-to-all(bf16[8,32,128]{2,1,0:T(8,128)(2,1)S(1)} %iterate.1), channel_id=1, replica_groups=mesh['groups'=2,'window'=4,'far'=2,'mid'=2,'near'=2,'cols'=4,'sub'=2] {'..., dimensions={0} | all-to-all | bytes 131072 | tf_op jit(solution)/shard_map/all_to_all | solution.py:263
  162.1 10.5 %all_to_all.35.got_ref = bf16[4,8,32,128]{3,2,1,0:T(8,128)(2,1)S(1)} all-to-all(bf16[4,8,32,128]{3,2,1,0:T(8,128)(2,1)S(1)} %broadcast_in_dim.8), channel_id=1, replica_groups=mesh['groups'=2,'window'=4,'far'=2,'mid'=2,'near'=2,'cols'=4,'sub'=2] {'..., dimensions={0} | all-to-all | bytes 524288 | tf_op jit(solution)/shard_map/all_to_all | solution.py:264
  172.6 0.8 unpack.1
  (5 shorter events, 0.1 us)
Async XLA Ops:
  0.0 81.5 %copy-start = (f32[4,32,1024]{2,1,0:T(8,128)S(1)}, f32[4,32,1024]{2,1,0:T(8,128)}, u32[]{:S(2)}) copy-start(f32[4,32,1024]{2,1,0:T(8,128)} %block_ref.1) | copy-start | bytes 1572868
  1.9 79.6 %copy-start.1 = (s32[4,1024]{1,0:T(4,128)S(1)}, s32[4,1024]{1,0:T(4,128)}, u32[]{:S(2)}) copy-start(s32[4,1024]{1,0:T(4,128)} %starts_ref.3) | copy-start | bytes 49156

commit v11 on v9

--- a/solution.py
+++ b/solution.py
@@ -29,11 +29,6 @@
 def split(a):
     high = a.astype(BF16)
     return high, (a - high.astype(F32)).astype(BF16)
-
-
-def dot3(a, b, dims):
-    (ah, al), (bh, bl) = split(a), split(b)
-    return dot(ah, bh, dims, None) + (dot(al, bh, dims, None) + dot(ah, bl, dims, None))
 
 
 def pack_kernel(returns_ref, starts_ref, out_ref):
@@ -81,19 +76,18 @@
     centered = jnp.where(live, values - mean, 0.0)
     squares = jnp.sum(centered * centered, axis=0, keepdims=True)
     scaled = centered * lax.rsqrt(squares + 1.0)
-    out_ref[0:total, :] = scaled
-    out_ref[total:, :] = block_ref[w, :, own].astype(BF16).astype(F32)
+    out_ref[0:total, :] = scaled.astype(BF16)
+    out_ref[total:, :] = block_ref[w, :, own].astype(BF16)
 
 
 def gram_kernel(both_ref, out_ref, all_ref):
     cores, rows, _ = both_ref.shape
     total = rows // LANES * LANES
     both = jnp.concatenate([both_ref[c] for c in range(cores)], axis=1)
-    high, low = split(both[:total])
-    rounded = both[total:].astype(BF16)
+    scaled, rounded = both[:total], both[total:]
     blocks = total // LANES
     across = ((1,), (1,))
-    proj = dot(rounded, high, across, None) + dot(rounded, low, across, None)
+    proj = dot(rounded, scaled, across, None)
     rest = []
     at = 0
 
@@ -104,8 +98,7 @@
 
     for a in range(blocks):
         here, on = slice(a * LANES, (a + 1) * LANES), slice(a * LANES, total)
-        strip = dot(high[here], high[on], across, None)
-        strip += dot(low[here], high[on], across, None) + dot(high[here], low[on], across, None)
+        strip = dot(scaled[here], scaled[on], across, None)
         put(strip[:HALF, :LANES])
         rest.append(strip[HALF:, :LANES])
         for b in range(1, blocks - a):
@@ -186,7 +179,9 @@
         moved = stacked[:factors] + (stacked[factors:] + dot(high, low_ref[...], inward, None))
         gram = dot(moved, proj, ((1,), (1,))) * (1.0 / assets)
         proj = dot(inverse_lower(gram), moved if step < ITERS - 1 else proj, inward)
-    loadings = dot3(proj, scaled_ref[0:total, :], inward).astype(BF16)
+    high, low = split(proj)
+    scaled = scaled_ref[0:total, :]
+    loadings = (dot(high, scaled, inward, None) + dot(low, scaled, inward, None)).astype(BF16)
     out_ref[...] = jnp.broadcast_to(loadings[None], out_ref.shape)
 
 
@@ -225,7 +220,7 @@
     height = (filled + unit - 1) // unit * unit
     scaled = pl.pallas_call(
         scale_kernel,
-        out_shape=jax.ShapeDtypeStruct((total + factors, LANES), F32),
+        out_shape=jax.ShapeDtypeStruct((total + factors, LANES), BF16),
         in_specs=[VMEM, VMEM, VMEM],
         out_specs=VMEM,
         compiler_params=PARAMS,

time: 170 us -> 169 us (level)
  no operation moved by 1% of the time
where the time goes in v11:
time: 169 us
  blocking collectives  160 us (95%)
  Pallas kernels  8.38 us (5%)
    all_to_all x1, blocking collectives, on_device(): got = lax.all_to_all(packed, ROWS, 0, 0, tiled=True)  79.6 us
    all_to_all x1, blocking collectives, on_device(): got = lax.all_to_all(sent, ('window', 'far'), 0, 0, tiled=True)  27.7 us
    all_to_all x1, blocking collectives, on_device(): lax.all_to_all(partial.reshape(pieces, share, LANES), block, 0, 0, tiled=...  12.8 us
    all_to_all x1, blocking collectives, on_device(): lax.all_to_all(jnp.broadcast_to(own[None], (pieces, share, LANES)), block...  10.2 us
    all_to_all x1, blocking collectives, on_device(): lax.all_to_all(jnp.broadcast_to(got[None], (NEAR, *got.shape)), quad, 0,...  10.2 us
    all_gather x1, blocking collectives, on_device(): own = lax.all_gather(own, 'far').sum(axis=0)  9.31 us
    all_gather x1, blocking collectives, on_device(): own = lax.all_gather(own, 'mid').sum(axis=0)  6.04 us
    pallas_call x1, Pallas kernels, on_device(): pl.pallas_call(functools.partial(iterate_kernel, assets), out_shape=jax.S...  4.87 us

profile of v11, /device:TPU:40, one launch (start us, length us, event | category | flops | bytes accessed | tf_op | source)
XLA Modules:
  0.0 168.7 jit_solution(13822507070758706062)
XLA Ops:
  0.0 0.0 copy-start
  0.0 1.9 %pack.1 = bf16[32,4,640]{2,1,0:T(4,128)(2,1)} custom-call(f32[4,16,1024]{2,1,0:T(8,128)} %returns_ref.1, s32[4,1024]{1,0:T(4,128)} %starts_ref.3), custom_call_target="tpu_custom_call" | custom-call | tf_op jit(solution)/shard_map/pack/pallas_call | solution.py:208
  1.9 0.0 copy-start.1
  1.9 79.6 %all_to_all.25.got_ref = bf16[32,4,640]{2,1,0:T(4,128)(2,1)S(1)} all-to-all(bf16[32,4,640]{2,1,0:T(4,128)(2,1)} %pack.1), channel_id=1, replica_groups=mesh['groups'=2,'window'=4,'far'=2,'mid'=2,'near'=2,'cols'=4,'sub'=2] {'..., dimensions={0} | all-to-all | bytes 327680 | tf_op jit(solution)/shard_map/all_to_all | solution.py:215
  81.5 0.0 copy-done
  81.5 0.0 copy-done.1
  81.5 0.3 scale.1.scaled_ref
  81.8 2.1 %all-gather = bf16[1088,128]{1,0:T(8,128)(2,1)S(1)} all-gather(bf16[544,128]{1,0:T(8,128)(2,1)S(1)} %scale.1.scaled_ref), channel_id=2, replica_groups=mesh['groups'=2,'window'=4,'far'=2,'mid'=2,'near'=2,'cols'=4,'sub'=2] {'..., dimensions={0}, use_global_device_ids=true | all-gather | bytes 417792 | tf_op jit(solution)/shard_map/all_gather | solution.py:229
  83.9 0.5 gram.1
  84.4 12.8 %all_to_all.26 = f32[8,80,128]{2,1,0:T(8,128)S(1)} all-to-all(f32[8,80,128]{2,1,0:T(8,128)S(1)} %bitcast.5), channel_id=1, replica_groups=mesh['groups'=2,'window'=4,'far'=2,'mid'=2,'near'=2,'cols'=4,'sub'=2] {'..., dimensions={0} | all-to-all | bytes 655360 | tf_op jit(solution)/shard_map/all_to_all | solution.py:242
  97.2 6.0 %all-gather.1 = f32[160,128]{1,0:T(8,128)S(1)} all-gather(f32[80,128]{1,0:T(8,128)S(1)} %reduce_sum.27), channel_id=3, replica_groups=mesh['groups'=2,'window'=4,'far'=2,'mid'=2,'near'=2,'cols'=4,'sub'=2] {'..., dimensions={0}, use_global_device_ids=true | all-gather | bytes 122880 | tf_op jit(solution)/shard_map/all_gather | solution.py:243
  103.2 9.3 %all-gather.2 = f32[160,128]{1,0:T(8,128)S(1)} all-gather(f32[80,128]{1,0:T(8,128)S(1)} %reduce_sum.28), channel_id=4, replica_groups=mesh['groups'=2,'window'=4,'far'=2,'mid'=2,'near'=2,'cols'=4,'sub'=2] {'..., dimensions={0}, use_global_device_ids=true | all-gather | bytes 122880 | tf_op jit(solution)/shard_map/all_gather | solution.py:244
  112.6 10.2 %all_to_all.27 = f32[8,80,128]{2,1,0:T(8,128)S(1)} all-to-all(f32[8,80,128]{2,1,0:T(8,128)S(1)} %broadcast_in_dim.4), channel_id=1, replica_groups=mesh['groups'=2,'window'=4,'far'=2,'mid'=2,'near'=2,'cols'=4,'sub'=2] {'..., dimensions={0} | all-to-all | bytes 655360 | tf_op jit(solution)/shard_map/all_to_all | solution.py:245
  122.8 2.3 %all_gather.27.got_ref = f32[1280,128]{1,0:T(8,128)S(1)} all-gather(f32[640,128]{1,0:T(8,128)S(1)} %bitcast.7), channel_id=1, replica_groups=mesh['groups'=2,'window'=4,'far'=2,'mid'=2,'near'=2,'cols'=4,'sub'=2] {'..., dimensions={0}, use_global_device_ids=true | all-gather | bytes 983040 | tf_op jit(solution)/shard_map/all_gather | solution.py:246
  125.1 4.9 %iterate.1 = bf16[8,32,128]{2,1,0:T(8,128)(2,1)S(1)} custom-call(f32[1280,128]{1,0:T(8,128)S(1)} %all_gather.27.got_ref, bf16[544,128]{1,0:T(8,128)(2,1)S(1)} %scale.1.scaled_ref), custom_call_target="tpu_custom_call" | custom-call | tf_op jit(solution)/shard_map/iterate/pallas_call | solution.py:249
  130.0 27.7 %all_to_all.28 = bf16[8,32,128]{2,1,0:T(8,128)(2,1)S(1)} all-to-all(bf16[8,32,128]{2,1,0:T(8,128)(2,1)S(1)} %iterate.1), channel_id=1, replica_groups=mesh['groups'=2,'window'=4,'far'=2,'mid'=2,'near'=2,'cols'=4,'sub'=2] {'..., dimensions={0} | all-to-all | bytes 131072 | tf_op jit(solution)/shard_map/all_to_all | solution.py:258
  157.7 10.2 %all_to_all.29.got_ref = bf16[4,8,32,128]{3,2,1,0:T(8,128)(2,1)S(1)} all-to-all(bf16[4,8,32,128]{3,2,1,0:T(8,128)(2,1)S(1)} %broadcast_in_dim.5), channel_id=1, replica_groups=mesh['groups'=2,'window'=4,'far'=2,'mid'=2,'near'=2,'cols'=4,'sub'=2] {'..., dimensions={0} | all-to-all | bytes 524288 | tf_op jit(solution)/shard_map/all_to_all | solution.py:259
  167.9 0.8 unpack.1
  (5 shorter events, 0.1 us)
Async XLA Ops:
  0.0 81.5 %copy-start = (f32[4,32,1024]{2,1,0:T(8,128)S(1)}, f32[4,32,1024]{2,1,0:T(8,128)}, u32[]{:S(2)}) copy-start(f32[4,32,1024]{2,1,0:T(8,128)} %block_ref.1) | copy-start | bytes 1572868
  1.9 79.6 %copy-start.1 = (s32[4,1024]{1,0:T(4,128)S(1)}, s32[4,1024]{1,0:T(4,128)}, u32[]{:S(2)}) copy-start(s32[4,1024]{1,0:T(4,128)} %starts_ref.3) | copy-start | bytes 49156

commit v12 on v11

--- a/solution.py
+++ b/solution.py
@@ -240,8 +240,8 @@
     pieces = lax.axis_size(block)
     share = height // sub // pieces
     own = lax.all_to_all(partial.reshape(pieces, share, LANES), block, 0, 0, tiled=True).sum(axis=0)
+    own = lax.all_gather(own, "far").sum(axis=0)
     own = lax.all_gather(own, "mid").sum(axis=0)
-    own = lax.all_gather(own, "far").sum(axis=0)
     own = lax.all_to_all(jnp.broadcast_to(own[None], (pieces, share, LANES)), block, 0, 0, tiled=True)
     whole = lax.all_gather(own.reshape(height // sub, LANES), "sub", tiled=True)
 

time: 169 us -> 170 us (level)
  no operation moved by 1% of the time
where the time goes in v12:
time: 170 us; the launch traced here: 169 us
  blocking collectives  161 us (95%)
  Pallas kernels  8.38 us (5%)
    all_to_all x1, blocking collectives, on_device(): got = lax.all_to_all(packed, ROWS, 0, 0, tiled=True)  79.6 us
    all_to_all x1, blocking collectives, on_device(): got = lax.all_to_all(sent, ('window', 'far'), 0, 0, tiled=True)  27.7 us
    all_to_all x1, blocking collectives, on_device(): lax.all_to_all(partial.reshape(pieces, share, LANES), block, 0, 0, tiled=...  12.8 us
    all_to_all x1, blocking collectives, on_device(): lax.all_to_all(jnp.broadcast_to(got[None], (NEAR, *got.shape)), quad, 0,...  10.7 us
    all_to_all x1, blocking collectives, on_device(): lax.all_to_all(jnp.broadcast_to(own[None], (pieces, share, LANES)), block...  10.2 us
    all_gather x1, blocking collectives, on_device(): own = lax.all_gather(own, 'far').sum(axis=0)  9.76 us
    all_gather x1, blocking collectives, on_device(): own = lax.all_gather(own, 'mid').sum(axis=0)  5.6 us
    pallas_call x1, Pallas kernels, on_device(): pl.pallas_call(functools.partial(iterate_kernel, assets), out_shape=jax.S...  4.87 us

profile of v12, /device:TPU:40, one launch (start us, length us, event | category | flops | bytes accessed | tf_op | source)
XLA Modules:
  0.0 169.2 jit_solution(8510602248589317888)
XLA Ops:
  0.0 0.0 copy-start
  0.0 1.9 %pack.1 = bf16[32,4,640]{2,1,0:T(4,128)(2,1)} custom-call(f32[4,16,1024]{2,1,0:T(8,128)} %returns_ref.1, s32[4,1024]{1,0:T(4,128)} %starts_ref.3), custom_call_target="tpu_custom_call" | custom-call | tf_op jit(solution)/shard_map/pack/pallas_call | solution.py:208
  1.9 0.0 copy-start.1
  1.9 79.6 %all_to_all.25.got_ref = bf16[32,4,640]{2,1,0:T(4,128)(2,1)S(1)} all-to-all(bf16[32,4,640]{2,1,0:T(4,128)(2,1)} %pack.1), channel_id=1, replica_groups=mesh['groups'=2,'window'=4,'far'=2,'mid'=2,'near'=2,'cols'=4,'sub'=2] {'..., dimensions={0} | all-to-all | bytes 327680 | tf_op jit(solution)/shard_map/all_to_all | solution.py:215
  81.5 0.0 copy-done
  81.5 0.0 copy-done.1
  81.5 0.3 scale.1.scaled_ref
  81.8 2.1 %all-gather = bf16[1088,128]{1,0:T(8,128)(2,1)S(1)} all-gather(bf16[544,128]{1,0:T(8,128)(2,1)S(1)} %scale.1.scaled_ref), channel_id=2, replica_groups=mesh['groups'=2,'window'=4,'far'=2,'mid'=2,'near'=2,'cols'=4,'sub'=2] {'..., dimensions={0}, use_global_device_ids=true | all-gather | bytes 417792 | tf_op jit(solution)/shard_map/all_gather | solution.py:229
  83.9 0.5 gram.1
  84.4 12.8 %all_to_all.26 = f32[8,80,128]{2,1,0:T(8,128)S(1)} all-to-all(f32[8,80,128]{2,1,0:T(8,128)S(1)} %bitcast.5), channel_id=1, replica_groups=mesh['groups'=2,'window'=4,'far'=2,'mid'=2,'near'=2,'cols'=4,'sub'=2] {'..., dimensions={0} | all-to-all | bytes 655360 | tf_op jit(solution)/shard_map/all_to_all | solution.py:242
  97.2 9.8 %all-gather.1 = f32[160,128]{1,0:T(8,128)S(1)} all-gather(f32[80,128]{1,0:T(8,128)S(1)} %reduce_sum.27), channel_id=3, replica_groups=mesh['groups'=2,'window'=4,'far'=2,'mid'=2,'near'=2,'cols'=4,'sub'=2] {'..., dimensions={0}, use_global_device_ids=true | all-gather | bytes 122880 | tf_op jit(solution)/shard_map/all_gather | solution.py:243
  106.9 5.6 %all-gather.2 = f32[160,128]{1,0:T(8,128)S(1)} all-gather(f32[80,128]{1,0:T(8,128)S(1)} %reduce_sum.28), channel_id=4, replica_groups=mesh['groups'=2,'window'=4,'far'=2,'mid'=2,'near'=2,'cols'=4,'sub'=2] {'..., dimensions={0}, use_global_device_ids=true | all-gather | bytes 122880 | tf_op jit(solution)/shard_map/all_gather | solution.py:244
  112.6 10.2 %all_to_all.27 = f32[8,80,128]{2,1,0:T(8,128)S(1)} all-to-all(f32[8,80,128]{2,1,0:T(8,128)S(1)} %broadcast_in_dim.4), channel_id=1, replica_groups=mesh['groups'=2,'window'=4,'far'=2,'mid'=2,'near'=2,'cols'=4,'sub'=2] {'..., dimensions={0} | all-to-all | bytes 655360 | tf_op jit(solution)/shard_map/all_to_all | solution.py:245
  122.8 2.3 %all_gather.27.got_ref = f32[1280,128]{1,0:T(8,128)S(1)} all-gather(f32[640,128]{1,0:T(8,128)S(1)} %bitcast.7), channel_id=1, replica_groups=mesh['groups'=2,'window'=4,'far'=2,'mid'=2,'near'=2,'cols'=4,'sub'=2] {'..., dimensions={0}, use_global_device_ids=true | all-gather | bytes 983040 | tf_op jit(solution)/shard_map/all_gather | solution.py:246
  125.1 4.9 %iterate.1 = bf16[8,32,128]{2,1,0:T(8,128)(2,1)S(1)} custom-call(f32[1280,128]{1,0:T(8,128)S(1)} %all_gather.27.got_ref, bf16[544,128]{1,0:T(8,128)(2,1)S(1)} %scale.1.scaled_ref), custom_call_target="tpu_custom_call" | custom-call | tf_op jit(solution)/shard_map/iterate/pallas_call | solution.py:249
  130.0 27.7 %all_to_all.28 = bf16[8,32,128]{2,1,0:T(8,128)(2,1)S(1)} all-to-all(bf16[8,32,128]{2,1,0:T(8,128)(2,1)S(1)} %iterate.1), channel_id=1, replica_groups=mesh['groups'=2,'window'=4,'far'=2,'mid'=2,'near'=2,'cols'=4,'sub'=2] {'..., dimensions={0} | all-to-all | bytes 131072 | tf_op jit(solution)/shard_map/all_to_all | solution.py:258
  157.7 10.7 %all_to_all.29.got_ref = bf16[4,8,32,128]{3,2,1,0:T(8,128)(2,1)S(1)} all-to-all(bf16[4,8,32,128]{3,2,1,0:T(8,128)(2,1)S(1)} %broadcast_in_dim.5), channel_id=1, replica_groups=mesh['groups'=2,'window'=4,'far'=2,'mid'=2,'near'=2,'cols'=4,'sub'=2] {'..., dimensions={0} | all-to-all | bytes 524288 | tf_op jit(solution)/shard_map/all_to_all | solution.py:259
  168.4 0.8 unpack.1
  (5 shorter events, 0.1 us)
Async XLA Ops:
  0.0 81.5 %copy-start = (f32[4,32,1024]{2,1,0:T(8,128)S(1)}, f32[4,32,1024]{2,1,0:T(8,128)}, u32[]{:S(2)}) copy-start(f32[4,32,1024]{2,1,0:T(8,128)} %block_ref.1) | copy-start | bytes 1572868
  1.9 79.6 %copy-start.1 = (s32[4,1024]{1,0:T(4,128)S(1)}, s32[4,1024]{1,0:T(4,128)}, u32[]{:S(2)}) copy-start(s32[4,1024]{1,0:T(4,128)} %starts_ref.3) | copy-start | bytes 49156

commit v13 on v11

--- a/solution.py
+++ b/solution.py
@@ -203,7 +203,7 @@
     sides = cols * sub
     total = days * rows
     assets = width * sides
-    quad, block = ("mid", "near"), ("near", "cols")
+    quad, block = ("mid", "near"), ("cols", "near")
 
     packed = pl.pallas_call(
         pack_kernel,

time: 169 us -> 169 us (level)
  no operation moved by 1% of the time
where the time goes in v13:
time: 169 us
  blocking collectives  160 us (95%)
  Pallas kernels  8.39 us (5%)
    all_to_all x1, blocking collectives, on_device(): got = lax.all_to_all(packed, ROWS, 0, 0, tiled=True)  79.6 us
    all_to_all x1, blocking collectives, on_device(): got = lax.all_to_all(sent, ('window', 'far'), 0, 0, tiled=True)  27.8 us
    all_to_all x1, blocking collectives, on_device(): lax.all_to_all(partial.reshape(pieces, share, LANES), block, 0, 0, tiled=...  12.8 us
    all_to_all x1, blocking collectives, on_device(): lax.all_to_all(jnp.broadcast_to(got[None], (NEAR, *got.shape)), quad, 0,...  10.2 us
    all_to_all x1, blocking collectives, on_device(): lax.all_to_all(jnp.broadcast_to(own[None], (pieces, share, LANES)), block...  10.2 us
    all_gather x1, blocking collectives, on_device(): own = lax.all_gather(own, 'far').sum(axis=0)  9.31 us
    all_gather x1, blocking collectives, on_device(): own = lax.all_gather(own, 'mid').sum(axis=0)  6.04 us
    pallas_call x1, Pallas kernels, on_device(): pl.pallas_call(functools.partial(iterate_kernel, assets), out_shape=jax.S...  4.87 us

profile of v13, /device:TPU:40, one launch (start us, length us, event | category | flops | bytes accessed | tf_op | source)
XLA Modules:
  0.0 168.9 jit_solution(9394506628579405600)
XLA Ops:
  0.0 0.0 copy-start
  0.0 1.9 %pack.1 = bf16[32,4,640]{2,1,0:T(4,128)(2,1)} custom-call(f32[4,16,1024]{2,1,0:T(8,128)} %returns_ref.1, s32[4,1024]{1,0:T(4,128)} %starts_ref.3), custom_call_target="tpu_custom_call" | custom-call | tf_op jit(solution)/shard_map/pack/pallas_call | solution.py:208
  1.9 0.0 copy-start.1
  1.9 79.6 %all_to_all.25.got_ref = bf16[32,4,640]{2,1,0:T(4,128)(2,1)S(1)} all-to-all(bf16[32,4,640]{2,1,0:T(4,128)(2,1)} %pack.1), channel_id=1, replica_groups=mesh['groups'=2,'window'=4,'far'=2,'mid'=2,'near'=2,'cols'=4,'sub'=2] {'..., dimensions={0} | all-to-all | bytes 327680 | tf_op jit(solution)/shard_map/all_to_all | solution.py:215
  81.5 0.0 copy-done
  81.5 0.0 copy-done.1
  81.5 0.3 scale.1.scaled_ref
  81.8 2.1 %all-gather = bf16[1088,128]{1,0:T(8,128)(2,1)S(1)} all-gather(bf16[544,128]{1,0:T(8,128)(2,1)S(1)} %scale.1.scaled_ref), channel_id=2, replica_groups=mesh['groups'=2,'window'=4,'far'=2,'mid'=2,'near'=2,'cols'=4,'sub'=2] {'..., dimensions={0}, use_global_device_ids=true | all-gather | bytes 417792 | tf_op jit(solution)/shard_map/all_gather | solution.py:229
  83.9 0.5 gram.1
  84.4 12.8 %all_to_all.26 = f32[8,80,128]{2,1,0:T(8,128)S(1)} all-to-all(f32[8,80,128]{2,1,0:T(8,128)S(1)} %bitcast.5), channel_id=1, replica_groups=mesh['groups'=2,'window'=4,'far'=2,'mid'=2,'near'=2,'cols'=4,'sub'=2] {'..., dimensions={0} | all-to-all | bytes 655360 | tf_op jit(solution)/shard_map/all_to_all | solution.py:242
  97.2 6.0 %all-gather.1 = f32[160,128]{1,0:T(8,128)S(1)} all-gather(f32[80,128]{1,0:T(8,128)S(1)} %reduce_sum.27), channel_id=3, replica_groups=mesh['groups'=2,'window'=4,'far'=2,'mid'=2,'near'=2,'cols'=4,'sub'=2] {'..., dimensions={0}, use_global_device_ids=true | all-gather | bytes 122880 | tf_op jit(solution)/shard_map/all_gather | solution.py:243
  103.2 9.3 %all-gather.2 = f32[160,128]{1,0:T(8,128)S(1)} all-gather(f32[80,128]{1,0:T(8,128)S(1)} %reduce_sum.28), channel_id=4, replica_groups=mesh['groups'=2,'window'=4,'far'=2,'mid'=2,'near'=2,'cols'=4,'sub'=2] {'..., dimensions={0}, use_global_device_ids=true | all-gather | bytes 122880 | tf_op jit(solution)/shard_map/all_gather | solution.py:244
  112.6 10.2 %all_to_all.27 = f32[8,80,128]{2,1,0:T(8,128)S(1)} all-to-all(f32[8,80,128]{2,1,0:T(8,128)S(1)} %broadcast_in_dim.4), channel_id=1, replica_groups=mesh['groups'=2,'window'=4,'far'=2,'mid'=2,'near'=2,'cols'=4,'sub'=2] {'..., dimensions={0} | all-to-all | bytes 655360 | tf_op jit(solution)/shard_map/all_to_all | solution.py:245
  122.8 2.3 %all_gather.27.got_ref = f32[1280,128]{1,0:T(8,128)S(1)} all-gather(f32[640,128]{1,0:T(8,128)S(1)} %bitcast.7), channel_id=1, replica_groups=mesh['groups'=2,'window'=4,'far'=2,'mid'=2,'near'=2,'cols'=4,'sub'=2] {'..., dimensions={0}, use_global_device_ids=true | all-gather | bytes 983040 | tf_op jit(solution)/shard_map/all_gather | solution.py:246
  125.1 4.9 %iterate.1 = bf16[8,32,128]{2,1,0:T(8,128)(2,1)S(1)} custom-call(f32[1280,128]{1,0:T(8,128)S(1)} %all_gather.27.got_ref, bf16[544,128]{1,0:T(8,128)(2,1)S(1)} %scale.1.scaled_ref), custom_call_target="tpu_custom_call" | custom-call | tf_op jit(solution)/shard_map/iterate/pallas_call | solution.py:249
  130.0 27.8 %all_to_all.28 = bf16[8,32,128]{2,1,0:T(8,128)(2,1)S(1)} all-to-all(bf16[8,32,128]{2,1,0:T(8,128)(2,1)S(1)} %iterate.1), channel_id=1, replica_groups=mesh['groups'=2,'window'=4,'far'=2,'mid'=2,'near'=2,'cols'=4,'sub'=2] {'..., dimensions={0} | all-to-all | bytes 131072 | tf_op jit(solution)/shard_map/all_to_all | solution.py:258
  157.8 10.2 %all_to_all.29.got_ref = bf16[4,8,32,128]{3,2,1,0:T(8,128)(2,1)S(1)} all-to-all(bf16[4,8,32,128]{3,2,1,0:T(8,128)(2,1)S(1)} %broadcast_in_dim.5), channel_id=1, replica_groups=mesh['groups'=2,'window'=4,'far'=2,'mid'=2,'near'=2,'cols'=4,'sub'=2] {'..., dimensions={0} | all-to-all | bytes 524288 | tf_op jit(solution)/shard_map/all_to_all | solution.py:259
  168.0 0.8 unpack.1
  (5 shorter events, 0.1 us)
Async XLA Ops:
  0.0 81.5 %copy-start = (f32[4,32,1024]{2,1,0:T(8,128)S(1)}, f32[4,32,1024]{2,1,0:T(8,128)}, u32[]{:S(2)}) copy-start(f32[4,32,1024]{2,1,0:T(8,128)} %block_ref.1) | copy-start | bytes 1572868
  1.9 79.6 %copy-start.1 = (s32[4,1024]{1,0:T(4,128)S(1)}, s32[4,1024]{1,0:T(4,128)}, u32[]{:S(2)}) copy-start(s32[4,1024]{1,0:T(4,128)} %starts_ref.3) | copy-start | bytes 49156

commit v14 on v13

--- a/solution.py
+++ b/solution.py
@@ -187,10 +187,10 @@
 
 def unpack_kernel(got_ref, out_ref):
     windows, _, width = out_ref.shape
-    near, blocks = got_ref.shape[:2]
+    near = got_ref.shape[0]
     for w in range(windows):
         for j in range(width // LANES):
-            block = w * (blocks // windows) + j // near
+            block = j // near * windows + w
             out_ref[w, :, j * LANES : (j + 1) * LANES] = got_ref[j % near, block].astype(F32)
 
 
@@ -255,7 +255,7 @@
         compiler_params=PARAMS,
         name="iterate",
     )(whole, scaled)
-    got = lax.all_to_all(sent, ("window", "far"), 0, 0, tiled=True)
+    got = lax.all_to_all(sent, ("far", "window"), 0, 0, tiled=True)
     got = lax.all_to_all(jnp.broadcast_to(got[None], (NEAR, *got.shape)), quad, 0, 0, tiled=True)
     return pl.pallas_call(
         unpack_kernel,

time: 169 us -> 169 us (level)
    all_to_all x1, blocking collectives: 27.8 us -> 24.8 us  [on_device(): got = lax.all_to_all(sent, ('far', 'window'), 0, 0, tiled=True)]
    all_to_all x1, blocking collectives: 10.2 us -> 13.1 us  [on_device(): lax.all_to_all(jnp.broadcast_to(got[None], (NEAR, *got.shape)), quad, 0,...]
where the time goes in v14:
time: 169 us
  blocking collectives  160 us (95%)
  Pallas kernels  8.39 us (5%)
    all_to_all x1, blocking collectives, on_device(): got = lax.all_to_all(packed, ROWS, 0, 0, tiled=True)  79.6 us
    all_to_all x1, blocking collectives, on_device(): got = lax.all_to_all(sent, ('far', 'window'), 0, 0, tiled=True)  24.8 us
    all_to_all x1, blocking collectives, on_device(): lax.all_to_all(jnp.broadcast_to(got[None], (NEAR, *got.shape)), quad, 0,...  13.1 us
    all_to_all x1, blocking collectives, on_device(): lax.all_to_all(partial.reshape(pieces, share, LANES), block, 0, 0, tiled=...  12.8 us
    all_to_all x1, blocking collectives, on_device(): lax.all_to_all(jnp.broadcast_to(own[None], (pieces, share, LANES)), block...  10.2 us
    all_gather x1, blocking collectives, on_device(): own = lax.all_gather(own, 'far').sum(axis=0)  9.31 us
    all_gather x1, blocking collectives, on_device(): own = lax.all_gather(own, 'mid').sum(axis=0)  6.04 us
    pallas_call x1, Pallas kernels, on_device(): pl.pallas_call(functools.partial(iterate_kernel, assets), out_shape=jax.S...  4.87 us

profile of v14, /device:TPU:40, one launch (start us, length us, event | category | flops | bytes accessed | tf_op | source)
XLA Modules:
  0.0 168.7 jit_solution(8302026752116426523)
XLA Ops:
  0.0 0.0 copy-start
  0.0 1.9 %pack.1 = bf16[32,4,640]{2,1,0:T(4,128)(2,1)} custom-call(f32[4,16,1024]{2,1,0:T(8,128)} %returns_ref.1, s32[4,1024]{1,0:T(4,128)} %starts_ref.3), custom_call_target="tpu_custom_call" | custom-call | tf_op jit(solution)/shard_map/pack/pallas_call | solution.py:208
  1.9 0.0 copy-start.1
  1.9 79.6 %all_to_all.25.got_ref = bf16[32,4,640]{2,1,0:T(4,128)(2,1)S(1)} all-to-all(bf16[32,4,640]{2,1,0:T(4,128)(2,1)} %pack.1), channel_id=1, replica_groups=mesh['groups'=2,'window'=4,'far'=2,'mid'=2,'near'=2,'cols'=4,'sub'=2] {'..., dimensions={0} | all-to-all | bytes 327680 | tf_op jit(solution)/shard_map/all_to_all | solution.py:215
  81.5 0.0 copy-done
  81.5 0.0 copy-done.1
  81.5 0.3 scale.1.scaled_ref
  81.8 2.1 %all-gather = bf16[1088,128]{1,0:T(8,128)(2,1)S(1)} all-gather(bf16[544,128]{1,0:T(8,128)(2,1)S(1)} %scale.1.scaled_ref), channel_id=2, replica_groups=mesh['groups'=2,'window'=4,'far'=2,'mid'=2,'near'=2,'cols'=4,'sub'=2] {'..., dimensions={0}, use_global_device_ids=true | all-gather | bytes 417792 | tf_op jit(solution)/shard_map/all_gather | solution.py:229
  83.9 0.5 gram.1
  84.4 12.8 %all_to_all.26 = f32[8,80,128]{2,1,0:T(8,128)S(1)} all-to-all(f32[8,80,128]{2,1,0:T(8,128)S(1)} %bitcast.5), channel_id=1, replica_groups=mesh['groups'=2,'window'=4,'far'=2,'mid'=2,'near'=2,'cols'=4,'sub'=2] {'..., dimensions={0} | all-to-all | bytes 655360 | tf_op jit(solution)/shard_map/all_to_all | solution.py:242
  97.2 6.0 %all-gather.1 = f32[160,128]{1,0:T(8,128)S(1)} all-gather(f32[80,128]{1,0:T(8,128)S(1)} %reduce_sum.27), channel_id=3, replica_groups=mesh['groups'=2,'window'=4,'far'=2,'mid'=2,'near'=2,'cols'=4,'sub'=2] {'..., dimensions={0}, use_global_device_ids=true | all-gather | bytes 122880 | tf_op jit(solution)/shard_map/all_gather | solution.py:243
  103.2 9.3 %all-gather.2 = f32[160,128]{1,0:T(8,128)S(1)} all-gather(f32[80,128]{1,0:T(8,128)S(1)} %reduce_sum.28), channel_id=4, replica_groups=mesh['groups'=2,'window'=4,'far'=2,'mid'=2,'near'=2,'cols'=4,'sub'=2] {'..., dimensions={0}, use_global_device_ids=true | all-gather | bytes 122880 | tf_op jit(solution)/shard_map/all_gather | solution.py:244
  112.6 10.2 %all_to_all.27 = f32[8,80,128]{2,1,0:T(8,128)S(1)} all-to-all(f32[8,80,128]{2,1,0:T(8,128)S(1)} %broadcast_in_dim.4), channel_id=1, replica_groups=mesh['groups'=2,'window'=4,'far'=2,'mid'=2,'near'=2,'cols'=4,'sub'=2] {'..., dimensions={0} | all-to-all | bytes 655360 | tf_op jit(solution)/shard_map/all_to_all | solution.py:245
  122.8 2.3 %all_gather.27.got_ref = f32[1280,128]{1,0:T(8,128)S(1)} all-gather(f32[640,128]{1,0:T(8,128)S(1)} %bitcast.7), channel_id=1, replica_groups=mesh['groups'=2,'window'=4,'far'=2,'mid'=2,'near'=2,'cols'=4,'sub'=2] {'..., dimensions={0}, use_global_device_ids=true | all-gather | bytes 983040 | tf_op jit(solution)/shard_map/all_gather | solution.py:246
  125.1 4.9 %iterate.1 = bf16[8,32,128]{2,1,0:T(8,128)(2,1)S(1)} custom-call(f32[1280,128]{1,0:T(8,128)S(1)} %all_gather.27.got_ref, bf16[544,128]{1,0:T(8,128)(2,1)S(1)} %scale.1.scaled_ref), custom_call_target="tpu_custom_call" | custom-call | tf_op jit(solution)/shard_map/iterate/pallas_call | solution.py:249
  130.0 24.8 %all_to_all.28 = bf16[8,32,128]{2,1,0:T(8,128)(2,1)S(1)} all-to-all(bf16[8,32,128]{2,1,0:T(8,128)(2,1)S(1)} %iterate.1), channel_id=1, replica_groups=mesh['groups'=2,'window'=4,'far'=2,'mid'=2,'near'=2,'cols'=4,'sub'=2] {'..., dimensions={0} | all-to-all | bytes 131072 | tf_op jit(solution)/shard_map/all_to_all | solution.py:258
  154.8 13.1 %all_to_all.29.got_ref = bf16[4,8,32,128]{3,2,1,0:T(8,128)(2,1)S(1)} all-to-all(bf16[4,8,32,128]{3,2,1,0:T(8,128)(2,1)S(1)} %broadcast_in_dim.5), channel_id=1, replica_groups=mesh['groups'=2,'window'=4,'far'=2,'mid'=2,'near'=2,'cols'=4,'sub'=2] {'..., dimensions={0} | all-to-all | bytes 524288 | tf_op jit(solution)/shard_map/all_to_all | solution.py:259
  167.9 0.8 unpack.1
  (5 shorter events, 0.1 us)
Async XLA Ops:
  0.0 81.5 %copy-start = (f32[4,32,1024]{2,1,0:T(8,128)S(1)}, f32[4,32,1024]{2,1,0:T(8,128)}, u32[]{:S(2)}) copy-start(f32[4,32,1024]{2,1,0:T(8,128)} %block_ref.1) | copy-start | bytes 1572868
  1.9 79.6 %copy-start.1 = (s32[4,1024]{1,0:T(4,128)S(1)}, s32[4,1024]{1,0:T(4,128)}, u32[]{:S(2)}) copy-start(s32[4,1024]{1,0:T(4,128)} %starts_ref.3) | copy-start | bytes 49156
